TPU v7x, 32 devices: a whole 2x2x4 slice. The times are simulated.
32 devices in a mesh: member: 2 (over y), blk: 16 (over z, x, core).
Axes of the slice: x: 2, y: 2, z: 4, core: 2. Of those that a mesh axis runs over, the one named last changes fastest.
Arguments:
- heat_anomaly: float32 [8, 1536, 512], P('member', 'blk'), parts along dimension 0, may hold values from -6 to 6
- saltiness_anomaly: float32 [8, 1536, 512], P('member', 'blk'), parts along dimension 0, may hold values from -6 to 6
- first_axis_flow: float32 [8, 1536, 512], P('member', 'blk'), parts along dimension 0, may hold values from -4 to 4
- second_axis_flow: float32 [8, 1536, 512], P('member', 'blk'), parts along dimension 0, may hold values from -4 to 4
- layer_spacing: float32 [4], replicated, may hold values from 0.5 to 4
- diagonal_shift: float32 [1536, 512], P('blk'), may hold values from 0.02 to 0.2
- water_tile_flags: int32 [16, 8], P('blk'), may hold values 0 or 1
Outputs:
- new_temperature: bfloat16 [8, 1536, 512], P('member', 'blk'), parts along dimension 0
- new_salinity: bfloat16 [8, 1536, 512], P('member', 'blk'), parts along dimension 0
- new_u: bfloat16 [8, 1536, 512], P('member', 'blk'), parts along dimension 0
- new_v: bfloat16 [8, 1536, 512], P('member', 'blk'), parts along dimension 0
- height: float32 [3072, 512], P(('member', 'blk')), parts along dimension 0
- residual: float32 [3072, 512], P(('member', 'blk')), parts along dimension 0
There are 2 independent parts, one for each index of `member`. A program takes and returns all parts, laid end to end along the dimension named above; an argument that names none is the same for every part. Nothing has to cross between parts.
Inputs may be any that keep to these rules, and one draw needn't show every extreme that they name: `water_tile_flags`: 1 marks an ocean block, 0 a land block.
All inputs are finite; a program needn't handle non-finite values.
Results may differ from a plain program's by a relative error of at most 0.001.
Values sent between devices are 32-bit elements; how exact they have to be, the bound alone decides.
No kernel may reach another device: no remote copies, remote signals or barrier semaphores. Data moves between devices by JAX's collectives and lax.ppermute only.
A program may use at most 128 MiB of HBM per device.

v0:
```python
import functools

import jax
import jax.numpy as jnp
from jax import lax
from jax.experimental import pallas as pl
from jax.experimental.pallas import tpu as pltpu
from jax.sharding import PartitionSpec as P

SSTEP = 4
CG_BLOCKS = 3
STEPS = SSTEP * CG_BLOCKS
COURANT = 0.2
PAD = 16
MARGIN = 8
BASE = PAD + MARGIN


def shift(value, amount, axis):
    return pltpu.roll(value, amount % value.shape[axis], axis)


def two_sum(a, b):
    s = a + b
    t = s - a
    return s, (a - (s - t)) + (b - t)


def fast_two_sum(a, b):
    s = a + b
    return s, b - (s - a)


def split(a):
    c = 4097.0 * a
    hi = c - (c - a)
    return hi, a - hi


def two_prod(a, b):
    p = a * b
    ah, al = split(a)
    bh, bl = split(b)
    return p, ((ah * bh - p) + ah * bl + al * bh) + al * bl


def pair_add(a, b):
    s, e = two_sum(a[0], b[0])
    return fast_two_sum(s, e + (a[1] + b[1]))


def pair_scale(a, c):
    p, e = two_prod(a[0], c)
    return p, e + a[1] * c


def upwind(speed, behind, ahead):
    return jnp.where(speed > 0.0, speed * behind, speed * ahead)


def face_speeds(u, v, east_wet, north_wet):
    east = 0.5 * (u + shift(u, -1, 0))[: 3 * MARGIN] * east_wet
    centre = v[MARGIN : 3 * MARGIN]
    north = 0.5 * (centre + shift(centre, -1, 1)) * north_wet
    return east, north


def advect(q, east, north, wet):
    east_flux = upwind(east, q[: 3 * MARGIN], shift(q, -1, 0)[: 3 * MARGIN])
    centre = q[MARGIN : 3 * MARGIN]
    north_flux = upwind(north, centre, shift(centre, -1, 1))
    spread = (east_flux - shift(east_flux, 1, 0))[MARGIN:] + (
        north_flux - shift(north_flux, 1, 1)
    )
    return wet * (centre - COURANT * spread)


def level_weight(spacing, level):
    total = spacing[0]
    for k in range(1, spacing.shape[0]):
        total = total + spacing[k]
    return spacing[level] / total


def north_wetness(wet):
    lane = lax.broadcasted_iota(jnp.int32, wet.shape, 1)
    return jnp.where(lane == wet.shape[1] - 1, 0.0, wet * shift(wet, -1, 1))


def inner_kernel(spacing, heat, salt, u, v, wet_ref, o_heat, o_salt, o_u, o_v, t_u, t_v):
    level = pl.program_id(0)
    width = u.shape[1]
    weight = level_weight(spacing, level)
    wet = wet_ref[0:1]
    wet8 = wet_ref[...]
    north_wet = north_wetness(wet8)[0:1]
    east_wet = wet * wet

    @pl.when(level == 0)
    def _():
        t_u[...] = jnp.zeros_like(t_u)
        t_v[...] = jnp.zeros_like(t_v)

    def strip(index, carry):
        start = pl.multiple_of(PAD + index * PAD, PAD)
        rows = pl.ds(pl.multiple_of(start - MARGIN, MARGIN), 4 * MARGIN)
        keep = pl.ds(start, PAD)
        qu = u[0, rows]
        qv = v[0, rows]
        east, north = face_speeds(qu, qv, east_wet, north_wet)
        au = advect(qu, east, north, wet)
        av = advect(qv, east, north, wet)
        o_u[0, keep] = au.astype(o_u.dtype)
        o_v[0, keep] = av.astype(o_v.dtype)
        t_u[keep] += weight * au
        t_v[keep] += weight * av
        o_heat[0, keep] = advect(heat[0, rows], east, north, wet).astype(o_heat.dtype)
        o_salt[0, keep] = advect(salt[0, rows], east, north, wet).astype(o_salt.dtype)
        return carry

    lax.fori_loop(0, width // PAD - 2, strip, 0)


def inner_advance(spacing, heat, salt, u, v, wet):
    levels, width, extent = u.shape
    block = pl.BlockSpec((1, width, extent), lambda k: (k, 0, 0))
    whole = pl.BlockSpec((width, extent), lambda k: (0, 0))
    tracer = jax.ShapeDtypeStruct(u.shape, jnp.bfloat16)
    plane = jax.ShapeDtypeStruct((width, extent), jnp.float32)
    return pl.pallas_call(
        inner_kernel,
        grid=(levels,),
        out_shape=[tracer] * 4 + [plane] * 2,
        in_specs=[pl.BlockSpec(memory_space=pltpu.SMEM)]
        + [block] * 4
        + [pl.BlockSpec(wet.shape, lambda k: (0, 0))],
        out_specs=[block] * 4 + [whole] * 2,
        cost_estimate=pl.CostEstimate(
            flops=10000000000, bytes_accessed=5000000, transcendentals=0
        ),
        name="inner_advance",
    )(spacing, heat, salt, u, v, wet)


def edge_kernel(
    spacing, heat, salt, u, v, damp, wet_ref, low, high, t_u, t_v, i_heat, i_salt, i_u, i_v,
    o_heat, o_salt, o_u, o_v, o_basis, o_sums,
    bands, tu, tv, ocean, diag, fields, corner, edge_out, acc, sems, out_sems, field_sems,
):
    levels, width, extent = u.shape
    span = width + 2 * BASE
    sources = (heat, salt, u, v)
    copies = []

    def fetch(src, dst):
        copy = pltpu.make_async_copy(src, dst, sems.at[len(copies)])
        copy.start()
        copies.append(copy)

    for side, message in ((0, low), (1, high)):
        fetch(message.at[2 * levels + 1], corner.at[side])
    for q in range(4):
        fetch(sources[q].at[:, 0:BASE], bands.at[q, 0, :, BASE : 2 * BASE])
        fetch(sources[q].at[:, width - BASE : width], bands.at[q, 1, :, 0:BASE])
    for side, message in ((0, low), (1, high)):
        rows = slice(MARGIN, BASE) if side == 0 else slice(BASE, BASE + PAD)
        fetch(message.at[0:levels], bands.at[2, side, :, rows])
        fetch(message.at[levels : 2 * levels], bands.at[3, side, :, rows])
    fetch(damp, diag.at[BASE : BASE + width])
    fetch(low.at[2 * levels], diag.at[MARGIN:BASE])
    fetch(high.at[2 * levels], diag.at[BASE + width : BASE + width + PAD])
    fetch(t_u.at[PAD : width - PAD], tu.at[BASE + PAD : BASE + width - PAD])
    fetch(t_v.at[PAD : width - PAD], tv.at[BASE + PAD : BASE + width - PAD])
    for copy in copies:
        copy.wait()

    wet8 = wet_ref[...]
    wet_low = corner[0, MARGIN:PAD]
    wet_high = corner[1, MARGIN:PAD]
    for block in range(span // MARGIN):
        value = wet8
        if block < BASE // MARGIN:
            value = wet_low
        if block >= (BASE + width) // MARGIN:
            value = wet_high
        ocean[block * MARGIN : (block + 1) * MARGIN] = value
    for q in range(2):
        for k in range(levels):
            row = q * levels + k
            bands[q, 0, k, BASE - 1 : BASE] = corner[0, row : row + 1]
            bands[q, 1, k, BASE : BASE + 1] = corner[1, row : row + 1]

    for side in range(2):
        first = 0 if side == 0 else width
        for place in range(2):
            start = MARGIN + place * PAD
            base = first + start
            owned = place == 1 - side
            wet = ocean[base : base + PAD]
            around = ocean[base - MARGIN : base + BASE]
            east_wet = (around * shift(around, -1, 0))[: 3 * MARGIN]
            north_wet = north_wetness(wet[:MARGIN])[0:1]

            def level_step(k, sums, side=side, start=start, owned=owned, wet=wet[0:1],
                           east_wet=east_wet, north_wet=north_wet):
                weight = level_weight(spacing, k)
                rows = slice(start - MARGIN, start + BASE)
                qu = bands[2, side, k, rows]
                qv = bands[3, side, k, rows]
                east, north = face_speeds(qu, qv, east_wet, north_wet)
                au = advect(qu, east, north, wet)
                av = advect(qv, east, north, wet)
                if owned:
                    edge_out[2, side, k] = au.astype(edge_out.dtype)
                    edge_out[3, side, k] = av.astype(edge_out.dtype)
                    for q in range(2):
                        edge_out[q, side, k] = advect(
                            bands[q, side, k, rows], east, north, wet
                        ).astype(edge_out.dtype)
                return sums[0] + weight * au, sums[1] + weight * av

            zero = jnp.zeros((PAD, extent), jnp.float32)
            su, sv = lax.fori_loop(0, levels, level_step, (zero, zero))
            tu[base : base + PAD] = su
            tv[base : base + PAD] = sv

    results = []
    for q, target in enumerate((o_heat, o_salt, o_u, o_v)):
        for side in range(2):
            first = 0 if side == 0 else width - PAD
            copy = pltpu.make_async_copy(
                edge_out.at[q, side], target.at[:, first : first + PAD], out_sems.at[2 * q + side]
            )
            copy.start()
            results.append(copy)

    lane = lax.broadcasted_iota(jnp.int32, (PAD, extent), 1)

    def north_of(x):
        return jnp.where(lane == extent - 1, 0.0, shift(x, -1, 1))

    def south_of(x):
        return jnp.where(lane == 0, 0.0, shift(x, 1, 1))

    strips = (width + 2 * PAD) // PAD
    none = jnp.zeros((MARGIN, 128), jnp.float32)

    def inner(a, b, total):
        product = a * b
        part = product[:MARGIN] + product[MARGIN:]
        pieces = [part[:, i : i + 128] for i in range(0, extent, 128)]
        while len(pieces) > 1:
            pieces = [x + y for x, y in zip(pieces[::2], pieces[1::2])]
        s, e = two_sum(total[0], pieces[0])
        return s, total[1] + e

    square = (none, none)
    for strip in range(strips):
        start = MARGIN + strip * PAD
        around = slice(start - MARGIN, start + BASE)
        keep = slice(start, start + PAD)
        wet = ocean[keep]
        flow = tu[around]
        east_part = (shift(flow, -1, 0) - shift(flow, 1, 0))[MARGIN:BASE]
        cross = tv[keep]
        start_field = wet * (0.5 * (east_part + (north_of(cross) - south_of(cross))))
        fields[0, keep] = jnp.zeros_like(start_field)
        fields[1, keep] = start_field
        diag[keep] = 0.5 * (wet * (6.0 + diag[keep]) + (1.0 - wet)) - 2.0
        if 0 < strip < strips - 1:
            square = inner(start_field, start_field, square)
    acc[0, 0:MARGIN] = square[0]
    acc[1, 0:MARGIN] = square[1]
    for row in range(2 * STEPS + 1, acc.shape[1] // MARGIN):
        acc[0, row * MARGIN : (row + 1) * MARGIN] = none
        acc[1, row * MARGIN : (row + 1) * MARGIN] = none

    def save(j):
        return pltpu.make_async_copy(
            fields.at[j + 1, BASE : BASE + width], o_basis.at[j], field_sems.at[j]
        )

    save(0).start()

    def basis_step(j, carry):
        scale = jnp.where(j == 0, 0.5, 1.0)
        mixed, square = (none, none), (none, none)
        for strip in range(strips):
            start = MARGIN + strip * PAD
            around = slice(start - MARGIN, start + BASE)
            keep = slice(start, start + PAD)
            wide = fields[j + 1, around]
            masked = wide * ocean[around]
            sides = (shift(masked, -1, 0) + shift(masked, 1, 0))[MARGIN:BASE]
            column = masked[MARGIN:BASE] + 0.5 * sides
            near = sides + (north_of(column) + south_of(column))
            centre = wide[MARGIN:BASE]
            image = diag[keep] * centre - (0.5 * ocean[keep]) * near
            following = scale * image - fields[j, keep]
            fields[j + 2, keep] = following
            if 0 < strip < strips - 1:
                mixed = inner(centre, following, mixed)
                square = inner(following, following, square)
        for place, value in ((2 * j + 1, mixed), (2 * j + 2, square)):
            at = pl.ds(pl.multiple_of(place * MARGIN, MARGIN), MARGIN)
            acc[0, at] = value[0]
            acc[1, at] = value[1]
        save(j + 1).start()
        return carry

    lax.fori_loop(0, STEPS, basis_step, 0)

    slots = acc.shape[1] // MARGIN
    pairs = [
        (acc[0, pl.ds(s, slots, stride=MARGIN)], acc[1, pl.ds(s, slots, stride=MARGIN)])
        for s in range(MARGIN)
    ]
    while len(pairs) > 1:
        pairs = [pair_add(x, y) for x, y in zip(pairs[::2], pairs[1::2])]
    total = pairs[0]
    step = 64
    while step:
        total = pair_add(total, (shift(total[0], step, 1), shift(total[1], step, 1)))
        step //= 2
    row = lax.broadcasted_iota(jnp.int32, (MARGIN, 128), 0)
    place = lax.broadcasted_iota(jnp.int32, (MARGIN, 128), 1)
    lined = []
    for part in total:
        merged = none
        for group in range(slots // MARGIN):
            merged = jnp.where(
                place // MARGIN == group, part[group * MARGIN : (group + 1) * MARGIN], merged
            )
        merged = jnp.where(place % MARGIN == row, merged, 0.0)
        for s in (4, 2, 1):
            merged = merged + shift(merged, s, 0)
        lined.append(merged)
    o_sums[...] = jnp.broadcast_to(jnp.where(row < 4, lined[0], lined[1])[None], o_sums.shape)
    for j in range(STEPS + 1):
        save(j).wait()
    for copy in results:
        copy.wait()


def edge_advance(spacing, heat, salt, u, v, damp, wet, low, high, inner, members):
    levels, width, extent = u.shape
    span = width + 2 * BASE
    slots = 32
    anywhere = pl.BlockSpec(memory_space=pl.ANY)
    tracer = jax.ShapeDtypeStruct(u.shape, jnp.bfloat16)
    f32 = jnp.float32
    return pl.pallas_call(
        edge_kernel,
        out_shape=[tracer] * 4
        + [
            jax.ShapeDtypeStruct((STEPS + 1, width, extent), f32),
            jax.ShapeDtypeStruct((members, MARGIN, 128), f32),
        ],
        in_specs=[pl.BlockSpec(memory_space=pltpu.SMEM)]
        + [anywhere] * 5
        + [pl.BlockSpec(memory_space=pltpu.VMEM)]
        + [anywhere] * 8,
        out_specs=[anywhere] * 5 + [pl.BlockSpec(memory_space=pltpu.VMEM)],
        scratch_shapes=[
            pltpu.VMEM((4, 2, levels, 2 * BASE, extent), f32),
            pltpu.VMEM((span, extent), f32),
            pltpu.VMEM((span, extent), f32),
            pltpu.VMEM((span, extent), f32),
            pltpu.VMEM((span, extent), f32),
            pltpu.VMEM((STEPS + 2, span, extent), f32),
            pltpu.VMEM((2, PAD, extent), f32),
            pltpu.VMEM((4, 2, levels, PAD, extent), jnp.bfloat16),
            pltpu.VMEM((2, slots * MARGIN, 128), f32),
            pltpu.SemaphoreType.DMA((24,)),
            pltpu.SemaphoreType.DMA((8,)),
            pltpu.SemaphoreType.DMA((STEPS + 1,)),
        ],
        input_output_aliases={11 + q: q for q in range(4)},
        cost_estimate=pl.CostEstimate(
            flops=10000000000, bytes_accessed=5000000, transcendentals=0
        ),
        name="edge_advance",
    )(spacing, heat, salt, u, v, damp, wet, low, high, inner[4], inner[5], *inner[:4])


def combine_kernel(sums, basis, height, resid, held, sems):
    copies = []
    for j in range(STEPS + 1):
        copy = pltpu.make_async_copy(basis.at[j], held.at[j], sems.at[j])
        copy.start()
        copies.append(copy)

    members = sums.shape[0]
    lane = lax.broadcasted_iota(jnp.int32, (MARGIN, 128), 1)
    row = lax.broadcasted_iota(jnp.int32, (MARGIN, 128), 0)
    pieces = [(sums[i], jnp.zeros((MARGIN, 128), jnp.float32)) for i in range(members)]
    while len(pieces) > 1:
        merged = []
        for x, y in zip(pieces[::2], pieces[1::2]):
            s, e = two_sum(x[0], y[0])
            merged.append((s, (x[1] + y[1]) + e))
        if len(pieces) % 2:
            merged.append(pieces[-1])
        pieces = merged
    total, error = pieces[0]
    other = shift(total, 4, 0)
    error_other = shift(error, 4, 0)
    upper = row < 4
    dots = fast_two_sum(
        jnp.where(upper, total, other),
        jnp.where(upper, other, total) + jnp.where(upper, error, error_other),
    )

    def at(x, k):
        return jnp.broadcast_to(x[:, k : k + 1], x.shape)

    odd = lane % 2 == 1
    anchor = tuple(jnp.where(odd, at(x, 1), at(x, 0)) for x in dots)
    moments = pair_add((2.0 * dots[0], 2.0 * dots[1]), (-anchor[0], -anchor[1]))
    inside = lane <= 2 * STEPS
    moments = tuple(jnp.where(inside, x, 0.0) for x in moments)

    def ahead(x):
        return shift(x, -1, 1)

    def behind(x):
        return shift(x, 1, 1)

    def image_of_products(x):
        after = tuple(ahead(c) for c in x)
        before = tuple(jnp.where(lane == 0, a, behind(c)) for a, c in zip(after, x))
        out = pair_add(pair_add(after, before), (2.0 * x[0], 2.0 * x[1]))
        return 0.25 * out[0], 0.25 * out[1]

    def image_of_coefficients(x):
        after = tuple(ahead(c) for c in x)
        before = tuple(
            jnp.where(lane == 0, 0.0, jnp.where(lane == 1, 2.0 * behind(c), behind(c))) for c in x
        )
        out = pair_add(pair_add(after, before), (2.0 * x[0], 2.0 * x[1]))
        return 0.25 * out[0], 0.25 * out[1]

    unit = jnp.where(lane == 0, 1.0, 0.0).astype(jnp.float32)
    zero = jnp.zeros_like(unit)
    r_products, p_products = moments, moments
    c_r, c_p, c_x = (unit, zero), (unit, zero), zero
    for k in range(STEPS):
        image = image_of_products(p_products)
        norm_now = at(r_products[0], k)
        alpha = norm_now / at(image[0], k)
        change = pair_scale(image, -alpha)
        r_products = pair_add(r_products, change)
        c_x = c_x + alpha * c_p[0]
        c_r = pair_add(c_r, pair_scale(image_of_coefficients(c_p), -alpha))
        if k + 1 < STEPS:
            lead = 0.5 if k == 0 else 0.25
            beta = (-lead * alpha) * at(r_products[0], k + 1) / norm_now
            p_products = pair_add(r_products, pair_scale(p_products, beta))
            c_p = pair_add(c_r, pair_scale(c_p, beta))

    width = height.shape[0]
    weights_x = [at(c_x, j)[0:1] for j in range(STEPS + 1)]
    weights_r = [at(c_r[0], j)[0:1] for j in range(STEPS + 1)]
    for copy in copies:
        copy.wait()
    for first in range(0, width, MARGIN):
        keep = slice(first, first + MARGIN)
        for left in range(0, height.shape[1], 128):
            cols = slice(left, left + 128)
            h = None
            for j in range(STEPS + 1):
                value = held[j, keep, cols]
                if h is None:
                    h, r = weights_x[0] * value, weights_r[0] * value
                else:
                    h, r = h + weights_x[j] * value, r + weights_r[j] * value
            height[keep, cols] = h
            resid[keep, cols] = r


def combine(sums, basis):
    plane = jax.ShapeDtypeStruct(basis.shape[1:], jnp.float32)
    return pl.pallas_call(
        combine_kernel,
        out_shape=[plane, plane],
        in_specs=[pl.BlockSpec(memory_space=pltpu.VMEM), pl.BlockSpec(memory_space=pl.ANY)],
        out_specs=[pl.BlockSpec(memory_space=pltpu.VMEM)] * 2,
        scratch_shapes=[
            pltpu.VMEM(basis.shape, jnp.float32),
            pltpu.SemaphoreType.DMA((STEPS + 1,)),
        ],
        name="combine",
    )(sums, basis)


def on_device(
    heat_anomaly,
    saltiness_anomaly,
    first_axis_flow,
    second_axis_flow,
    layer_spacing,
    diagonal_shift,
    water_tile_flags,
):
    members = lax.axis_size("blk")
    width, extent = diagonal_shift.shape
    fields = (heat_anomaly, saltiness_anomaly, first_axis_flow, second_axis_flow)
    wet = jnp.broadcast_to(
        jnp.repeat(
            water_tile_flags.astype(jnp.float32), extent // water_tile_flags.shape[1], axis=1
        ),
        (MARGIN, extent),
    )

    def message(first, edge):
        rows = slice(first, first + PAD)
        corner = jnp.concatenate(
            [
                heat_anomaly[:, edge],
                saltiness_anomaly[:, edge],
                wet,
            ],
            axis=0,
        )
        return jnp.concatenate(
            [
                first_axis_flow[:, rows],
                second_axis_flow[:, rows],
                diagonal_shift[rows][None],
                corner[None],
            ],
            axis=0,
        )

    forward = [(i, (i + 1) % members) for i in range(members)]
    backward = [(target, source) for source, target in forward]
    low = lax.ppermute(message(width - PAD, width - 1), "blk", forward)
    high = lax.ppermute(message(0, 0), "blk", backward)
    inner = inner_advance(layer_spacing, *fields, wet)
    *tracers, basis, sums = edge_advance(
        layer_spacing, *fields, diagonal_shift, wet, low, high, inner, members
    )
    gathered = lax.all_to_all(sums, "blk", 0, 0)
    height, resid = combine(gathered, basis)
    return (*tracers, height, resid)


def solution(mesh):
    columns = P("member", "blk", None)
    return jax.shard_map(
        on_device,
        mesh=mesh,
        in_specs=(columns, columns, columns, columns, P(), P("blk", None), P("blk", None)),
        out_specs=(
            columns,
            columns,
            columns,
            columns,
            P(("member", "blk"), None),
            P(("member", "blk"), None),
        ),
        check_vma=False,
    )
```

profile of v0, /device:TPU:0, one launch (start us, length us, event | category | flops | bytes accessed | tf_op | source)
XLA Modules:
  0.0 47.5 jit_solution(17111872623333427398)
XLA Ops:
  0.6 0.7 %convert_bitcast_fusion = f32[8]{0:T(128)S(1)} fusion(s32[1,8]{1,0:T(1,128)} %param.13), kind=kLoop, calls=%fused_computation.12 | loop fusion | flops 8 | bytes 64 | tf_op jit(solution)/shard_map/convert_element_type | solution.py:510
  1.3 0.1 broadcast_in_dim.22
  1.4 0.1 broadcast_in_dim.23
  1.4 0.9 %fusion.4 = (f32[4,1,512]{2,1,0:T(1,128)S(1)}, f32[4,1,512]{2,1,0:T(1,128)S(1)}) fusion(f32[4,96,512]{2,1,0:T(8,128)} %heat.3), kind=kLoop, calls=%fused_computation.15 | loop fusion | bytes 32768 | tf_op jit(solution)/shard_map/slice | solution.py:519
  2.3 0.9 %fusion.5 = (f32[4,1,512]{2,1,0:T(1,128)S(1)}, f32[4,1,512]{2,1,0:T(1,128)S(1)}) fusion(f32[4,96,512]{2,1,0:T(8,128)} %salt.3), kind=kLoop, calls=%fused_computation.16 | loop fusion | bytes 32768 | tf_op jit(solution)/shard_map/slice | solution.py:520
  3.2 0.8 %slice_bitcast_fusion = (f32[1,16,512]{2,1,0:T(8,128)S(1)}, f32[1,16,512]{2,1,0:T(8,128)S(1)}) fusion(f32[96,512]{1,0:T(8,128)} %damp.1), kind=kLoop, calls=%fused_computation.6 | loop fusion | bytes 131072 | tf_op jit(solution)/shard_map/broadcast_in_dim | solution.py:529
  4.0 1.1 %fusion.2 = (f32[4,16,512]{2,1,0:T(8,128)S(1)}, f32[4,16,512]{2,1,0:T(8,128)S(1)}, f32[4,16,512]{2,1,0:T(8,128)S(1)}, f32[4,16,512]{2,1,0:T(8,128)S(1)}) fusion(f32[4,96,512]{2,1,0:T(8,128)} %u.3, f32[4,96,512]{2,1,0:T(8,128)} %v.3), kind=kLoop, calls=%fused_computation.13 | loop fusion | bytes 1048576 | tf_op jit(solution)/shard_map/slice | solution.py:527
  5.2 0.0 copy-start
  5.2 0.5 %collective-permute-start = (f32[10,16,512]{2,1,0:T(8,128)S(1)}, f32[10,16,512]{2,1,0:T(8,128)S(1)}, u32[]{:S(2)}, u32[]{:S(2)}) collective-permute-start(f32[10,16,512]{2,1,0:T(8,128)S(1)} %pad_maximum_fusion), channel_id=1, source_target_pairs={{0,1},{1,2},{2,3},{3,4},{4,5},{5,6},{6,7},{7,8},{8,9},{9,10},{10,1... | collective-permute-start | bytes 983048 | tf_op jit(solution)/shard_map/ppermute | solution.py:537
  5.8 5.0 %collective-permute-start.1 = (f32[10,16,512]{2,1,0:T(8,128)S(1)}, f32[10,16,512]{2,1,0:T(8,128)S(1)}, u32[]{:S(2)}, u32[]{:S(2)}) collective-permute-start(f32[10,16,512]{2,1,0:T(8,128)S(1)} %pad_maximum_fusion.1), channel_id=1, source_target_pairs={{1,0},{2,1},{3,2},{4,3},{5,4},{6,5},{7,6},{8,7},{9,8},{10,9},{11,1... | collective-permute-start | bytes 983048 | tf_op jit(solution)/shard_map/ppermute | solution.py:538
  10.8 0.0 copy-done
  10.8 6.1 %inner_advance.1 = (bf16[4,96,512]{2,1,0:T(8,128)(2,1)}, bf16[4,96,512]{2,1,0:T(8,128)(2,1)}, bf16[4,96,512]{2,1,0:T(8,128)(2,1)}, bf16[4,96,512]{2,1,0:T(8,128)...) custom-call(f32[4]{0:T(128)} %spacing.3, f32[4,96,512]{2,1,0:T(8,128)} %heat.3, f32[4,96,512]{2,1,0:T(8,128)} %salt.3, ...), custom_call_target="tpu_custom_call" | custom-call | flops 10000000000 | bytes 5000000 | tf_op jit(solution)/shard_map/inner_advance/pallas_call | solution.py:130
  17.0 0.0 collective-permute-done.low
  17.0 0.0 copy-start.1
  17.0 0.0 collective-permute-done.1.high
  17.0 0.0 copy-start.2
  17.0 0.7 %copy-done.1 = f32[10,16,512]{2,1,0:T(8,128)} copy-done((f32[10,16,512]{2,1,0:T(8,128)}, f32[10,16,512]{2,1,0:T(8,128)S(1)}, u32[]{:S(2)}) %copy-start.1) | copy-done | bytes 327704
  17.7 0.1 copy-done.2
  17.8 10.5 %edge_advance.1 = (bf16[4,96,512]{2,1,0:T(8,128)(2,1)}, bf16[4,96,512]{2,1,0:T(8,128)(2,1)}, bf16[4,96,512]{2,1,0:T(8,128)(2,1)}, bf16[4,96,512]{2,1,0:T(8,128)(...) custom-call(f32[4]{0:T(128)} %spacing.3, ...), custom_call_target="tpu_custom_call", output_to_operand_aliasing={{0}: (11, {}), {1}: (12, {}), {2}: (13, {}), {3}: (14, {})} | custom-call | flops 10000000000 | bytes 5000000 | tf_op jit(solution)/shard_map/edge_advance/pallas_call | solution.py:352
  28.4 12.7 %all_to_all.5.sums = f32[16,8,128]{2,1,0:T(8,128)} all-to-all(f32[16,8,128]{2,1,0:T(8,128)} %get-tuple-element.30), channel_id=1, replica_groups=mesh['member'=2,'blk'=16] {'blk'}, dimensions={0} | all-to-all | bytes 131072 | tf_op jit(solution)/shard_map/all_to_all | solution.py:543
  41.1 6.4 %combine.1 = (f32[96,512]{1,0:T(8,128)}, f32[96,512]{1,0:T(8,128)}) custom-call(f32[16,8,128]{2,1,0:T(8,128)} %all_to_all.5.sums, f32[13,96,512]{2,1,0:T(8,128)} %get-tuple-element.31.basis), custom_call_target="tpu_custom_call" | custom-call | tf_op jit(solution)/shard_map/combine/pallas_call | solution.py:483
  (6 shorter events, 0.1 us)
Async XLA Ops:
  5.2 5.7 %copy-start = (f32[8,512]{1,0:T(8,128)}, f32[8,512]{1,0:T(8,128)S(1)}, u32[]{:S(2)}) copy-start(f32[8,512]{1,0:T(8,128)S(1)} %broadcast_in_dim.24.wet_ref) | copy-start | bytes 49156
  5.2 11.7 %collective-permute-start = (f32[10,16,512]{2,1,0:T(8,128)S(1)}, f32[10,16,512]{2,1,0:T(8,128)S(1)}, u32[]{:S(2)}, u32[]{:S(2)}) collective-permute-start(f32[10,16,512]{2,1,0:T(8,128)S(1)} %pad_maximum_fusion), channel_id=1, source_target_pairs={{0,1},{1,2},{2,3},{3,4},{4,5},{5,6},{6,7},{7,8},{8,9},{9,10},{10,1... | collective-permute-start | bytes 983048 | tf_op jit(solution)/shard_map/ppermute | solution.py:537
  5.8 11.2 %collective-permute-start.1 = (f32[10,16,512]{2,1,0:T(8,128)S(1)}, f32[10,16,512]{2,1,0:T(8,128)S(1)}, u32[]{:S(2)}, u32[]{:S(2)}) collective-permute-start(f32[10,16,512]{2,1,0:T(8,128)S(1)} %pad_maximum_fusion.1), channel_id=1, source_target_pairs={{1,0},{2,1},{3,2},{4,3},{5,4},{6,5},{7,6},{8,7},{9,8},{10,9},{11,1... | collective-permute-start | bytes 983048 | tf_op jit(solution)/shard_map/ppermute | solution.py:538
  17.0 0.7 %copy-start.1 = (f32[10,16,512]{2,1,0:T(8,128)}, f32[10,16,512]{2,1,0:T(8,128)S(1)}, u32[]{:S(2)}) copy-start(f32[10,16,512]{2,1,0:T(8,128)S(1)} %collective-permute-done.low) | copy-start | bytes 983044
  17.0 0.8 %copy-start.2 = (f32[10,16,512]{2,1,0:T(8,128)}, f32[10,16,512]{2,1,0:T(8,128)S(1)}, u32[]{:S(2)}) copy-start(f32[10,16,512]{2,1,0:T(8,128)S(1)} %collective-permute-done.1.high) | copy-start | bytes 983044
where the time goes:
time: 48.2 us; the launch traced here: 47.5 us
  Pallas kernels  23.1 us (48%)
  blocking collectives  12.7 us (26%)
  starting transfers between devices  5.57 us (12%)
  local copies, waits for them, and re-layouts  4.68 us (10%)
  between operations  0.74 us (2%)
  other arithmetic  0.72 us (1%)
    all_to_all x1, blocking collectives, on_device(): gathered = lax.all_to_all(sums, 'blk', 0, 0)  12.7 us
    pallas_call x1, Pallas kernels, edge_advance(): pl.pallas_call(edge_kernel, out_shape=[tracer] * 4 + [jax.ShapeDtypeStruc...  10.5 us
    pallas_call x1, Pallas kernels, combine(): pl.pallas_call(combine_kernel, out_shape=[plane, plane], in_specs=[pl.Blo...  6.45 us
    pallas_call x1, Pallas kernels, inner_advance(): pl.pallas_call(inner_kernel, grid=(levels,), out_shape=[tracer] * 4 + [pl...  6.13 us
    ppermute x1, starting transfers between devices, on_device(): high = lax.ppermute(message(0, 0), 'blk', backward)  5.02 us
    slice x1, local copies, waits for them, and re-layouts, message(): first_axis_flow[:, rows]  1.14 us
  transfers between devices with their start and end apart: 2, of which 0 were waited for; matrix products, arithmetic and copies ran while one was open for 0% of the time, Pallas kernels for 13%

commit v1 on v0

v1 whole, which is shorter than its diff:
```python
import functools

import jax
import jax.numpy as jnp
from jax import lax
from jax.experimental import pallas as pl
from jax.experimental.pallas import tpu as pltpu
from jax.sharding import PartitionSpec as P

SSTEP = 4
CG_BLOCKS = 3
STEPS = SSTEP * CG_BLOCKS
COURANT = 0.2
PAD = 16
MARGIN = 8
BASE = PAD + MARGIN
KIB = 1024
VMEM_BYTES = 65472 * KIB
PACK_ROOM = 10740 * KIB
INNER_ROOM = 12660 * KIB
EDGE_ROOM = 45 * KIB * KIB


def shift(value, amount, axis):
    return pltpu.roll(value, amount % value.shape[axis], axis)


def two_sum(a, b):
    s = a + b
    t = s - a
    return s, (a - (s - t)) + (b - t)


def fast_two_sum(a, b):
    s = a + b
    return s, b - (s - a)


def split(a):
    c = 4097.0 * a
    hi = c - (c - a)
    return hi, a - hi


def two_prod(a, b):
    p = a * b
    ah, al = split(a)
    bh, bl = split(b)
    return p, ((ah * bh - p) + ah * bl + al * bh) + al * bl


def pair_add(a, b):
    s, e = two_sum(a[0], b[0])
    return fast_two_sum(s, e + (a[1] + b[1]))


def pair_scale(a, c):
    p, e = two_prod(a[0], c)
    return p, e + a[1] * c


def upwind(speed, behind, ahead):
    return jnp.where(speed > 0.0, speed * behind, speed * ahead)


def face_speeds(u, v, east_wet, north_wet):
    east = 0.5 * (u + shift(u, -1, 0))[:-MARGIN] * east_wet
    centre = v[MARGIN:-MARGIN]
    north = 0.5 * (centre + shift(centre, -1, 1)) * north_wet
    return east, north


def advect(q, east, north, wet):
    east_flux = upwind(east, q[:-MARGIN], shift(q, -1, 0)[:-MARGIN])
    centre = q[MARGIN:-MARGIN]
    north_flux = upwind(north, centre, shift(centre, -1, 1))
    spread = (east_flux - shift(east_flux, 1, 0))[MARGIN:] + (
        north_flux - shift(north_flux, 1, 1)
    )
    return wet * (centre - COURANT * spread)


def lanes(shape):
    return lax.broadcasted_iota(jnp.int32, shape, 1)


def rows_in(shape):
    return lax.broadcasted_iota(jnp.int32, shape, 0)


def north_of(x):
    return jnp.where(lanes(x.shape) == x.shape[1] - 1, 0.0, shift(x, -1, 1))


def south_of(x):
    return jnp.where(lanes(x.shape) == 0, 0.0, shift(x, 1, 1))


def north_wetness(wet):
    return wet * north_of(wet)


def divergence(wet, flow, cross):
    east_part = shift(flow, -1, 0) - shift(flow, 1, 0)
    return wet * (0.5 * (east_part + (north_of(cross) - south_of(cross))))


def spacing_total(spacing):
    total = spacing[0]
    for k in range(1, spacing.shape[0]):
        total = total + spacing[k]
    return total


def pack_kernel(
    flags, spacing, heat, salt, u, v, damp, o_low, o_high, o_table, o_damp, windows, tips, sems
):
    levels, width, extent = u.shape
    tiles = flags.shape[1]
    messages = (o_high, o_low)
    copies = []
    for end in range(2):
        rows = pl.ds(0 if end == 0 else width - BASE, BASE)
        into = pl.ds(MARGIN if end == 0 else 0, BASE)
        tip = pl.ds(0 if end == 0 else width - MARGIN, MARGIN)
        for src, dst in (
            (u.at[:, rows], windows.at[0, end, :, into]),
            (v.at[:, rows], windows.at[1, end, :, into]),
            (heat.at[:, tip], tips.at[0, end]),
            (salt.at[:, tip], tips.at[1, end]),
        ):
            copy = pltpu.make_async_copy(src, dst, sems.at[len(copies)])
            copy.start()
            copies.append(copy)
    copy = pltpu.make_async_copy(damp, o_damp, sems.at[len(copies)])
    copy.start()
    copies.append(copy)
    lane = lanes((MARGIN, extent))
    wet = jnp.zeros((MARGIN, extent), jnp.float32)
    for tile in range(tiles):
        inside = (lane >= tile * (extent // tiles)) & (lane < (tile + 1) * (extent // tiles))
        wet = jnp.where(inside, flags[0, tile].astype(jnp.float32), wet)
    o_table[0:MARGIN] = wet
    wet_row = wet[0:1]
    east_wet = wet_row * wet_row
    north_wet = north_wetness(wet)[0:1]
    total = spacing_total(spacing)
    row = rows_in((MARGIN, extent))
    weights = jnp.zeros((MARGIN, extent), jnp.float32)
    for k in range(levels):
        weights = jnp.where(row == k, spacing[k], weights)
    o_table[MARGIN:PAD] = weights / total
    for copy in copies:
        copy.wait()
    for end in range(2):
        message = messages[end]

        def level_step(k, sums, end=end):
            weight = o_table[pl.ds(MARGIN + k, 1)]
            qu = windows[0, end, k]
            qv = windows[1, end, k]
            east, north = face_speeds(qu, qv, east_wet, north_wet)
            au = advect(qu, east, north, wet_row)
            av = advect(qv, east, north, wet_row)
            return sums[0] + weight * au, sums[1] + weight * av

        zero = jnp.zeros((PAD, extent), jnp.float32)
        flow, cross = lax.fori_loop(0, levels, level_step, (zero, zero))
        message[0] = divergence(wet_row, flow, cross)
        first = 0 if end == 0 else width - PAD
        message[1] = o_damp[first : first + PAD]
        for q in range(2):
            merged = jnp.zeros((MARGIN, extent), jnp.float32)
            for k in range(levels):
                if end == 0:
                    piece = shift(windows[q, 0, k, MARGIN:PAD], 2 * k, 0)
                else:
                    piece = shift(windows[q, 1, k, PAD:BASE], 2 * k + 2 - MARGIN, 0)
                merged = jnp.where(row // 2 == k, piece, merged)
            message[2, q * MARGIN : (q + 1) * MARGIN] = merged
        merged = jnp.zeros((MARGIN, extent), jnp.float32)
        for q in range(2):
            for k in range(levels):
                place = q * levels + k
                piece = shift(tips[q, end, k], place if end == 0 else place + 1, 0)
                merged = jnp.where(row == place, piece, merged)
        message[3, 0:MARGIN] = merged
        if end == 0:
            flow_piece = shift(flow[:MARGIN], -1, 0)
            cross_piece = shift(cross[:MARGIN], 1, 0)
        else:
            flow_piece = shift(flow[MARGIN:], -5, 0)
            cross_piece = shift(cross[MARGIN:], -4, 0)
        message[3, MARGIN:PAD] = jnp.where(
            row < 2, flow_piece, jnp.where(row == 2, cross_piece, wet)
        )


def pack(flags, spacing, heat, salt, u, v, damp):
    levels, width, extent = u.shape
    message = jax.ShapeDtypeStruct((4, PAD, extent), jnp.float32)
    smem = pl.BlockSpec(memory_space=pltpu.SMEM)
    return pl.pallas_call(
        pack_kernel,
        out_shape=[
            message,
            message,
            jax.ShapeDtypeStruct((PAD, extent), jnp.float32),
            jax.ShapeDtypeStruct(damp.shape, jnp.float32),
        ],
        in_specs=[smem, smem] + [pl.BlockSpec(memory_space=pl.ANY)] * 5,
        out_specs=[pl.BlockSpec(memory_space=pltpu.VMEM)] * 4,
        scratch_shapes=[
            pltpu.VMEM((2, 2, levels, 2 * PAD, extent), jnp.float32),
            pltpu.VMEM((2, 2, levels, MARGIN, extent), jnp.float32),
            pltpu.SemaphoreType.DMA((9,)),
        ],
        compiler_params=pltpu.CompilerParams(vmem_limit_bytes=VMEM_BYTES - PACK_ROOM),
        name="pack",
    )(flags, spacing, heat, salt, u, v, damp)


def inner_kernel(
    heat, salt, u, v, table,
    o_heat, o_salt, o_u, o_v, r_heat, r_salt, r_u, r_v, o_edge, o_start,
    bands, staged, tu, tv, sems, out_sems,
):
    levels, width, extent = u.shape
    sources = (heat, salt, u, v)
    targets = (o_heat, o_salt, o_u, o_v)
    rims = (r_heat, r_salt, r_u, r_v)
    inside = width - 2 * PAD

    def load(q, k):
        return pltpu.make_async_copy(
            sources[q].at[k], bands.at[q, k, pl.ds(MARGIN, width)], sems.at[q, k]
        )

    def store(q, k):
        return pltpu.make_async_copy(
            staged.at[q, k, pl.ds(PAD, inside)],
            targets[q].at[k, pl.ds(PAD, inside)],
            out_sems.at[q, k],
        )

    for k in range(levels):
        for q in (2, 3, 0, 1):
            load(q, k).start()
    wet = table[0:1]
    north_wet = north_wetness(table[0:MARGIN])[0:1]
    east_wet = wet * wet
    tu[...] = jnp.zeros_like(tu)
    tv[...] = jnp.zeros_like(tv)

    def level_step(k, carry):
        weight = table[pl.ds(MARGIN + k, 1)]
        for q in (2, 3, 0, 1):
            load(q, k).wait()

        def strip(index, carry):
            local = pl.ds(pl.multiple_of(index * PAD, PAD), PAD)
            later = pl.ds(pl.multiple_of(index * PAD + MARGIN, MARGIN), PAD)
            rows = pl.ds(pl.multiple_of(index * PAD, MARGIN), 2 * PAD)
            qu = bands[2, k, rows]
            qv = bands[3, k, rows]
            east, north = face_speeds(qu, qv, east_wet, north_wet)
            au = advect(qu, east, north, wet)
            av = advect(qv, east, north, wet)
            staged[2, k, local] = au.astype(staged.dtype)
            staged[3, k, local] = av.astype(staged.dtype)
            tu[later] += weight * au
            tv[later] += weight * av
            staged[0, k, local] = advect(bands[0, k, rows], east, north, wet).astype(staged.dtype)
            staged[1, k, local] = advect(bands[1, k, rows], east, north, wet).astype(staged.dtype)
            return carry

        lax.fori_loop(0, width // PAD, strip, 0)
        for q in range(4):
            store(q, k).start()
            rims[q][0, k] = bands[q, k, MARGIN:BASE]
            rims[q][1, k] = bands[q, k, width - MARGIN : width + MARGIN]
            o_edge[q, 0, k] = staged[q, k, 0:PAD]
            o_edge[q, 1, k] = staged[q, k, width - PAD : width]
        return carry

    lax.fori_loop(0, levels, level_step, 0)
    for first in range(0, width, PAD):
        keep = slice(first, first + PAD)
        flow = tu[first : first + 2 * PAD]
        cross = tv[first + MARGIN : first + BASE]
        east_part = (shift(flow, -1, 0) - shift(flow, 1, 0))[MARGIN:BASE]
        o_start[keep] = wet * (0.5 * (east_part + (north_of(cross) - south_of(cross))))
    for k in range(levels):
        for q in range(4):
            store(q, k).wait()


def inner_advance(heat, salt, u, v, table):
    levels, width, extent = u.shape
    f32 = jnp.float32
    tracer = jax.ShapeDtypeStruct(u.shape, jnp.bfloat16)
    plane = jax.ShapeDtypeStruct((width, extent), f32)
    vmem = pl.BlockSpec(memory_space=pltpu.VMEM)
    anywhere = pl.BlockSpec(memory_space=pl.ANY)
    return pl.pallas_call(
        inner_kernel,
        out_shape=[tracer] * 4
        + [jax.ShapeDtypeStruct((2, levels, PAD, extent), f32)] * 4
        + [jax.ShapeDtypeStruct((4, 2, levels, PAD, extent), jnp.bfloat16), plane],
        in_specs=[anywhere] * 4 + [vmem],
        out_specs=[anywhere] * 4 + [vmem] * 6,
        scratch_shapes=[
            pltpu.VMEM((4, levels, width + PAD, extent), f32),
            pltpu.VMEM((4, levels, width, extent), jnp.bfloat16),
            pltpu.VMEM((width + PAD, extent), f32),
            pltpu.VMEM((width + PAD, extent), f32),
            pltpu.SemaphoreType.DMA((4, levels)),
            pltpu.SemaphoreType.DMA((4, levels)),
        ],
        cost_estimate=pl.CostEstimate(
            flops=10000000000, bytes_accessed=5000000, transcendentals=0
        ),
        compiler_params=pltpu.CompilerParams(vmem_limit_bytes=VMEM_BYTES - INNER_ROOM),
        name="inner_advance",
    )(heat, salt, u, v, table)


def edge_kernel(
    r_heat, r_salt, r_u, r_v, edge_in, start_in, damp, table, low, high, i_heat, i_salt, i_u, i_v,
    o_heat, o_salt, o_u, o_v, fields, o_sums,
    ocean, diag, edge_out, acc, out_sems,
):
    rims = (r_heat, r_salt, r_u, r_v)
    levels, extent = r_u.shape[1], r_u.shape[3]
    width = start_in.shape[0]
    span = width + 2 * BASE
    wet8 = table[0:MARGIN]
    row = rows_in((MARGIN, extent))
    for block in range(BASE // MARGIN, (BASE + width) // MARGIN):
        ocean[block * MARGIN : (block + 1) * MARGIN] = wet8
    diag[BASE : BASE + width] = (
        0.5 * (table[0:1] * (6.0 + damp[...]) + (1.0 - table[0:1])) - 2.0
    )
    fields[1, BASE : BASE + width] = start_in[...]

    for side, message in ((0, low), (1, high)):
        wet_out = jnp.broadcast_to(message[3, PAD - 1 : PAD], (MARGIN, extent))
        outer = 0 if side == 0 else BASE + width
        for block in range(BASE // MARGIN):
            ocean[outer + block * MARGIN : outer + (block + 1) * MARGIN] = wet_out
        halo = MARGIN if side == 0 else BASE + width
        wet_row = wet_out[0:1]
        diag[halo : halo + PAD] = 0.5 * (
            wet_row * (6.0 + message[1]) + (1.0 - wet_row)
        ) - 2.0
        if side == 0:
            around = jnp.concatenate([wet_out, wet8, wet8], axis=0)
            beyond = jnp.concatenate([wet_out, wet_out, wet8], axis=0)
        else:
            around = jnp.concatenate([wet8, wet8, wet_out], axis=0)
            beyond = jnp.concatenate([wet8, wet_out, wet_out], axis=0)
        east_own = (around * shift(around, -1, 0))[:PAD]
        east_out = (beyond * shift(beyond, -1, 0))[:PAD]
        north_own = north_wetness(wet8)
        north_out = north_wetness(wet_out)

        def level_step(k, sums, side=side, message=message, east_own=east_own,
                       east_out=east_out, north_own=north_own, north_out=north_out,
                       wet_out=wet_out):
            weight = table[pl.ds(MARGIN + k, 1)]
            own, out = [], []
            for q in (2, 3):
                pair = message[2, (q - 2) * MARGIN : (q - 1) * MARGIN]
                mine = rims[q][side, k]
                if side == 0:
                    piece = pltpu.roll(pair, MARGIN - 2 - 2 * k, 0)
                    own.append(jnp.concatenate([piece, mine], axis=0))
                    out.append(jnp.concatenate([piece, piece, mine[:MARGIN]], axis=0))
                else:
                    piece = pltpu.roll(pair, (MARGIN - 2 * k) % MARGIN, 0)
                    own.append(jnp.concatenate([mine, piece], axis=0))
                    out.append(jnp.concatenate([mine[MARGIN:], piece, piece], axis=0))
            east, north = face_speeds(own[0], own[1], east_own, north_own)
            au = advect(own[0], east, north, wet8)
            av = advect(own[1], east, north, wet8)
            fresh = [None, None, au, av]
            for q in range(2):
                mine = rims[q][side, k]
                single = message[3, 0:MARGIN]
                place = q * levels + k
                if side == 0:
                    piece = pltpu.roll(single, (2 * MARGIN - 1 - place) % MARGIN, 0)
                    window = jnp.concatenate([piece, mine], axis=0)
                else:
                    piece = pltpu.roll(single, (MARGIN - place) % MARGIN, 0)
                    window = jnp.concatenate([mine, piece], axis=0)
                fresh[q] = advect(window, east, north, wet8)
            for q in range(4):
                old = edge_in[q, side, k].astype(jnp.float32)
                if side == 0:
                    value = jnp.concatenate([fresh[q], old[MARGIN:]], axis=0)
                else:
                    value = jnp.concatenate([old[:MARGIN], fresh[q]], axis=0)
                edge_out[q, side, k] = value.astype(edge_out.dtype)
            east, north = face_speeds(out[0], out[1], east_out, north_out)
            bu = advect(out[0], east, north, wet_out)
            bv = advect(out[1], east, north, wet_out)
            return (
                sums[0] + weight * au,
                sums[1] + weight * av,
                sums[2] + weight * bu,
                sums[3] + weight * bv,
            )

        zero = jnp.zeros((MARGIN, extent), jnp.float32)
        flow, cross, flow_out, cross_out = lax.fori_loop(
            0, levels, level_step, (zero, zero, zero, zero)
        )
        known = message[3, MARGIN:PAD]
        given = message[0]
        if side == 0:
            flow_out = jnp.where(row == MARGIN - 1, flow_out, shift(known, 5, 0))
            cross_out = jnp.where(row == MARGIN - 1, cross_out, shift(known, 4, 0))
            whole = divergence(
                jnp.concatenate([wet_out, wet8], axis=0),
                jnp.concatenate([flow_out, flow], axis=0),
                jnp.concatenate([cross_out, cross], axis=0),
            )
            fields[1, MARGIN : 2 * MARGIN] = given[:MARGIN]
            fields[1, 2 * MARGIN : BASE] = jnp.where(
                row >= MARGIN - 2, whole[:MARGIN], given[MARGIN:]
            )
            fields[1, BASE : BASE + MARGIN] = jnp.where(
                row < 2, whole[MARGIN:], start_in[0:MARGIN]
            )
        else:
            flow_out = jnp.where(row == 0, flow_out, shift(known, 1, 0))
            cross_out = jnp.where(row == 0, cross_out, shift(known, -1, 0))
            whole = divergence(
                jnp.concatenate([wet8, wet_out], axis=0),
                jnp.concatenate([flow, flow_out], axis=0),
                jnp.concatenate([cross, cross_out], axis=0),
            )
            top = BASE + width
            fields[1, top - MARGIN : top] = jnp.where(
                row >= MARGIN - 2, whole[:MARGIN], start_in[width - MARGIN : width]
            )
            fields[1, top : top + MARGIN] = jnp.where(row < 2, whole[MARGIN:], given[:MARGIN])
            fields[1, top + MARGIN : top + PAD] = given[MARGIN:]

    results = []
    for q, target in enumerate((o_heat, o_salt, o_u, o_v)):
        for side in range(2):
            first = 0 if side == 0 else width - PAD
            copy = pltpu.make_async_copy(
                edge_out.at[q, side],
                target.at[:, pl.ds(first, PAD)],
                out_sems.at[2 * q + side],
            )
            copy.start()
            results.append(copy)

    strips = (width + 2 * PAD) // PAD
    none = jnp.zeros((MARGIN, 128), jnp.float32)

    def inner(a, b, total):
        product = a * b
        part = product[:MARGIN] + product[MARGIN:]
        pieces = [part[:, i : i + 128] for i in range(0, extent, 128)]
        while len(pieces) > 1:
            pieces = [x + y for x, y in zip(pieces[::2], pieces[1::2])]
        s, e = two_sum(total[0], pieces[0])
        return s, total[1] + e

    square = (none, none)
    for strip in range(strips):
        keep = slice(MARGIN + strip * PAD, BASE + strip * PAD)
        fields[0, keep] = jnp.zeros((PAD, extent), jnp.float32)
        if 0 < strip < strips - 1:
            value = fields[1, keep]
            square = inner(value, value, square)
    acc[0, 0:MARGIN] = square[0]
    acc[1, 0:MARGIN] = square[1]
    for slot in range(2 * STEPS + 1, acc.shape[1] // MARGIN):
        acc[0, slot * MARGIN : (slot + 1) * MARGIN] = none
        acc[1, slot * MARGIN : (slot + 1) * MARGIN] = none

    def basis_step(j, carry):
        scale = jnp.where(j == 0, 0.5, 1.0)
        mixed, square = (none, none), (none, none)
        for strip in range(strips):
            start = MARGIN + strip * PAD
            around = slice(start - MARGIN, start + BASE)
            keep = slice(start, start + PAD)
            wide = fields[j + 1, around]
            masked = wide * ocean[around]
            sides = (shift(masked, -1, 0) + shift(masked, 1, 0))[MARGIN:BASE]
            column = masked[MARGIN:BASE] + 0.5 * sides
            near = sides + (north_of(column) + south_of(column))
            centre = wide[MARGIN:BASE]
            image = diag[keep] * centre - (0.5 * ocean[keep]) * near
            following = scale * image - fields[j, keep]
            fields[j + 2, keep] = following
            if 0 < strip < strips - 1:
                mixed = inner(centre, following, mixed)
                square = inner(following, following, square)
        for place, value in ((2 * j + 1, mixed), (2 * j + 2, square)):
            at = pl.ds(pl.multiple_of(place * MARGIN, MARGIN), MARGIN)
            acc[0, at] = value[0]
            acc[1, at] = value[1]
        return carry

    lax.fori_loop(0, STEPS, basis_step, 0)

    slots = acc.shape[1] // MARGIN
    pairs = [
        (acc[0, pl.ds(s, slots, stride=MARGIN)], acc[1, pl.ds(s, slots, stride=MARGIN)])
        for s in range(MARGIN)
    ]
    while len(pairs) > 1:
        pairs = [pair_add(x, y) for x, y in zip(pairs[::2], pairs[1::2])]
    total = pairs[0]
    step = 64
    while step:
        total = pair_add(total, (shift(total[0], step, 1), shift(total[1], step, 1)))
        step //= 2
    row = lax.broadcasted_iota(jnp.int32, (MARGIN, 128), 0)
    place = lax.broadcasted_iota(jnp.int32, (MARGIN, 128), 1)
    lined = []
    for part in total:
        merged = none
        for group in range(slots // MARGIN):
            merged = jnp.where(
                place // MARGIN == group, part[group * MARGIN : (group + 1) * MARGIN], merged
            )
        merged = jnp.where(place % MARGIN == row, merged, 0.0)
        for s in (4, 2, 1):
            merged = merged + shift(merged, s, 0)
        lined.append(merged)
    o_sums[...] = jnp.broadcast_to(jnp.where(row < 4, lined[0], lined[1])[None], o_sums.shape)
    for copy in results:
        copy.wait()


def edge_advance(damp, table, low, high, inner, members):
    *tracers, r_heat, r_salt, r_u, r_v, edge, start = inner
    levels, width, extent = tracers[0].shape
    span = width + 2 * BASE
    slots = 32
    anywhere = pl.BlockSpec(memory_space=pl.ANY)
    vmem = pl.BlockSpec(memory_space=pltpu.VMEM)
    tracer = jax.ShapeDtypeStruct(tracers[0].shape, jnp.bfloat16)
    f32 = jnp.float32
    return pl.pallas_call(
        edge_kernel,
        out_shape=[tracer] * 4
        + [
            jax.ShapeDtypeStruct((STEPS + 2, span, extent), f32),
            jax.ShapeDtypeStruct((members, MARGIN, 128), f32),
        ],
        in_specs=[vmem] * 10 + [anywhere] * 4,
        out_specs=[anywhere] * 4 + [vmem] * 2,
        scratch_shapes=[
            pltpu.VMEM((span, extent), f32),
            pltpu.VMEM((span, extent), f32),
            pltpu.VMEM((4, 2, levels, PAD, extent), jnp.bfloat16),
            pltpu.VMEM((2, slots * MARGIN, 128), f32),
            pltpu.SemaphoreType.DMA((8,)),
        ],
        input_output_aliases={10 + q: q for q in range(4)},
        cost_estimate=pl.CostEstimate(
            flops=10000000000, bytes_accessed=5000000, transcendentals=0
        ),
        compiler_params=pltpu.CompilerParams(vmem_limit_bytes=VMEM_BYTES - EDGE_ROOM),
        name="edge_advance",
    )(r_heat, r_salt, r_u, r_v, edge, start, damp, table, low, high, *tracers)


def combine_kernel(sums, fields, height, resid):
    members = sums.shape[0]
    lane = lax.broadcasted_iota(jnp.int32, (MARGIN, 128), 1)
    row = lax.broadcasted_iota(jnp.int32, (MARGIN, 128), 0)
    pieces = [(sums[i], jnp.zeros((MARGIN, 128), jnp.float32)) for i in range(members)]
    while len(pieces) > 1:
        merged = []
        for x, y in zip(pieces[::2], pieces[1::2]):
            s, e = two_sum(x[0], y[0])
            merged.append((s, (x[1] + y[1]) + e))
        if len(pieces) % 2:
            merged.append(pieces[-1])
        pieces = merged
    total, error = pieces[0]
    other = shift(total, 4, 0)
    error_other = shift(error, 4, 0)
    upper = row < 4
    dots = fast_two_sum(
        jnp.where(upper, total, other),
        jnp.where(upper, other, total) + jnp.where(upper, error, error_other),
    )

    def at(x, k):
        return jnp.broadcast_to(x[:, k : k + 1], x.shape)

    odd = lane % 2 == 1
    anchor = tuple(jnp.where(odd, at(x, 1), at(x, 0)) for x in dots)
    moments = pair_add((2.0 * dots[0], 2.0 * dots[1]), (-anchor[0], -anchor[1]))
    inside = lane <= 2 * STEPS
    moments = tuple(jnp.where(inside, x, 0.0) for x in moments)

    def ahead(x):
        return shift(x, -1, 1)

    def behind(x):
        return shift(x, 1, 1)

    def image_of_products(x):
        after = tuple(ahead(c) for c in x)
        before = tuple(jnp.where(lane == 0, a, behind(c)) for a, c in zip(after, x))
        out = pair_add(pair_add(after, before), (2.0 * x[0], 2.0 * x[1]))
        return 0.25 * out[0], 0.25 * out[1]

    def image_of_coefficients(x):
        after = tuple(ahead(c) for c in x)
        before = tuple(
            jnp.where(lane == 0, 0.0, jnp.where(lane == 1, 2.0 * behind(c), behind(c))) for c in x
        )
        out = pair_add(pair_add(after, before), (2.0 * x[0], 2.0 * x[1]))
        return 0.25 * out[0], 0.25 * out[1]

    unit = jnp.where(lane == 0, 1.0, 0.0).astype(jnp.float32)
    zero = jnp.zeros_like(unit)
    r_products, p_products = moments, moments
    c_r, c_p, c_x = (unit, zero), (unit, zero), zero
    for k in range(STEPS):
        image = image_of_products(p_products)
        norm_now = at(r_products[0], k)
        alpha = norm_now / at(image[0], k)
        change = pair_scale(image, -alpha)
        r_products = pair_add(r_products, change)
        c_x = c_x + alpha * c_p[0]
        c_r = pair_add(c_r, pair_scale(image_of_coefficients(c_p), -alpha))
        if k + 1 < STEPS:
            lead = 0.5 if k == 0 else 0.25
            beta = (-lead * alpha) * at(r_products[0], k + 1) / norm_now
            p_products = pair_add(r_products, pair_scale(p_products, beta))
            c_p = pair_add(c_r, pair_scale(c_p, beta))

    width = height.shape[0]
    weights_x = [at(c_x, j)[0:1] for j in range(STEPS + 1)]
    weights_r = [at(c_r[0], j)[0:1] for j in range(STEPS + 1)]
    for first in range(0, width, MARGIN):
        keep = slice(first, first + MARGIN)
        wide = slice(BASE + first, BASE + first + MARGIN)
        for left in range(0, height.shape[1], 128):
            cols = slice(left, left + 128)
            h = None
            for j in range(STEPS + 1):
                value = fields[j + 1, wide, cols]
                if h is None:
                    h, r = weights_x[0] * value, weights_r[0] * value
                else:
                    h, r = h + weights_x[j] * value, r + weights_r[j] * value
            height[keep, cols] = h
            resid[keep, cols] = r


def combine(sums, fields, width):
    plane = jax.ShapeDtypeStruct((width, fields.shape[2]), jnp.float32)
    vmem = pl.BlockSpec(memory_space=pltpu.VMEM)
    return pl.pallas_call(
        combine_kernel,
        out_shape=[plane, plane],
        in_specs=[vmem, vmem],
        out_specs=[vmem, vmem],
        compiler_params=pltpu.CompilerParams(vmem_limit_bytes=8 * 1024 * 1024),
        name="combine",
    )(sums, fields)


def on_device(
    heat_anomaly,
    saltiness_anomaly,
    first_axis_flow,
    second_axis_flow,
    layer_spacing,
    diagonal_shift,
    water_tile_flags,
):
    members = lax.axis_size("blk")
    fields = (heat_anomaly, saltiness_anomaly, first_axis_flow, second_axis_flow)
    to_next, to_last, table, damp = pack(water_tile_flags, layer_spacing, *fields, diagonal_shift)
    forward = [(i, (i + 1) % members) for i in range(members)]
    backward = [(target, source) for source, target in forward]
    low = lax.ppermute(to_next, "blk", forward)
    high = lax.ppermute(to_last, "blk", backward)
    inner = inner_advance(*fields, table)
    *tracers, basis, sums = edge_advance(damp, table, low, high, inner, members)
    gathered = lax.all_to_all(sums, "blk", 0, 0)
    height, resid = combine(gathered, basis, diagonal_shift.shape[0])
    return (*tracers, height, resid)


def solution(mesh):
    columns = P("member", "blk", None)
    return jax.shard_map(
        on_device,
        mesh=mesh,
        in_specs=(columns, columns, columns, columns, P(), P("blk", None), P("blk", None)),
        out_specs=(
            columns,
            columns,
            columns,
            columns,
            P(("member", "blk"), None),
            P(("member", "blk"), None),
        ),
        check_vma=False,
    )
```

time: 48.2 us -> 38.1 us (0.79)
  local copies, waits for them, and re-layouts: 4.68 us -> 1.3 us
  Pallas kernels: 23.1 us -> 20 us
  blocking collectives: 12.7 us -> 10.3 us
  other arithmetic: 0.72 us -> 0 us
    pallas_call x1, Pallas kernels: 10.5 us -> 5.2 us  [edge_advance(): pl.pallas_call(edge_kernel, out_shape=[tracer] * 4 + [jax.ShapeDtypeStruc...]
    slice x3 -> x0, local copies, waits for them, and re-layouts: 2.91 us -> none  [the longest x1 1.14 us: message(): first_axis_flow[:, rows]]
    all_to_all x1, blocking collectives: 12.7 us -> 10.3 us  [on_device(): gathered = lax.all_to_all(sums, 'blk', 0, 0)]
    pallas_call x2 -> x3, Pallas kernels: 12.6 us -> 14.8 us  [the longest x1 6.99 us: inner_advance(): pl.pallas_call(inner_kernel, out_shape=[tracer] * 4 + [jax.ShapeDtypeStru...]
    broadcast_in_dim x4 -> x0, local copies, waits for them, and re-layouts: 0.94 us -> none  [the longest x1 0.78 us: message(): diagonal_shift[rows][None]]
    convert_element_type x1 -> x0, other arithmetic: 0.66 us -> none  [on_device(): water_tile_flags.astype(jnp.float32)]
    unnamed x6 -> x4, local copies, waits for them, and re-layouts: 0.82 us -> 1.3 us
  transfers between devices with their start and end apart: 2 -> 2, of which waited for: 0 -> 0; matrix products, arithmetic and copies ran while one was open for 0% -> 0% of each run, Pallas kernels for 13% -> 18%
where the time goes in v1:
time: 38.1 us; the launch traced here: 37.9 us
  Pallas kernels  20 us (52%)
  blocking collectives  10.3 us (27%)
  starting transfers between devices  5.56 us (15%)
  local copies, waits for them, and re-layouts  1.3 us (3%)
  between operations  0.68 us (2%)
    all_to_all x1, blocking collectives, on_device(): gathered = lax.all_to_all(sums, 'blk', 0, 0)  10.3 us
    pallas_call x1, Pallas kernels, inner_advance(): pl.pallas_call(inner_kernel, out_shape=[tracer] * 4 + [jax.ShapeDtypeStru...  6.99 us
    pallas_call x1, Pallas kernels, edge_advance(): pl.pallas_call(edge_kernel, out_shape=[tracer] * 4 + [jax.ShapeDtypeStruc...  5.2 us
    ppermute x1, starting transfers between devices, on_device(): high = lax.ppermute(to_last, 'blk', backward)  5.02 us
    pallas_call x1, Pallas kernels, combine(): pl.pallas_call(combine_kernel, out_shape=[plane, plane], in_specs=[vmem,...  4.23 us
    pallas_call x1, Pallas kernels, pack(): pl.pallas_call(pack_kernel, out_shape=[message, message, jax.ShapeDtypeSt...  3.56 us
    unnamed x4, local copies, waits for them, and re-layouts  1.3 us
  transfers between devices with their start and end apart: 2, of which 0 were waited for; matrix products, arithmetic and copies ran while one was open for 0% of the time, Pallas kernels for 18%

profile of v1, /device:TPU:0, one launch (start us, length us, event | category | flops | bytes accessed | tf_op | source)
XLA Modules:
  0.0 37.9 jit_solution(12557793707357437820)
XLA Ops:
  0.6 0.0 copy-start
  0.6 0.6 %copy-done = s32[1,8]{1,0:T(1,128)S(1)} copy-done((s32[1,8]{1,0:T(1,128)S(1)}, s32[1,8]{1,0:T(1,128)}, u32[]{:S(2)}) %copy-start) | copy-done | bytes 56
  1.3 0.0 copy-start.1
  1.3 0.7 %copy-done.1 = f32[4]{0:T(128)S(1)} copy-done((f32[4]{0:T(128)S(1)}, f32[4]{0:T(128)}, u32[]{:S(2)}) %copy-start.1) | copy-done | bytes 40
  1.9 3.6 %pack.1 = (f32[4,16,512]{2,1,0:T(8,128)S(1)}, f32[4,16,512]{2,1,0:T(8,128)S(1)}, f32[16,512]{1,0:T(8,128)S(1)}, f32[96,512]{1,0:T(8,128)S(1)}) custom-call(s32[1,8]{1,0:T(1,128)S(1)} %copy-done, f32[4]{0:T(128)S(1)} %copy-done.1, f32[4,96,512]{2,1,0:T(8,128)} %heat.3, f32[4,96,512]{2,1,0:T(8,128)} %salt.3, f32[4,96,512]{2,1,0:T(8,128)} %u.3, ...), custom_call_target="tpu_custom_call" | custom-call | tf_op jit(solution)/shard_map/pack/pallas_call | solution.py:203
  5.5 0.5 %collective-permute-start = (f32[4,16,512]{2,1,0:T(8,128)S(1)}, f32[4,16,512]{2,1,0:T(8,128)S(1)}, u32[]{:S(2)}, u32[]{:S(2)}) collective-permute-start(f32[4,16,512]{2,1,0:T(8,128)S(1)} %get-tuple-element.36), channel_id=1, source_target_pairs={{0,1},{1,2},{2,3},{3,4},{4,5},{5,6},{6,7},{7,8},{8,9},{9,10},{10,1... | collective-permute-start | bytes 393224 | tf_op jit(solution)/shard_map/ppermute | solution.py:694
  6.1 5.0 %collective-permute-start.1 = (f32[4,16,512]{2,1,0:T(8,128)S(1)}, f32[4,16,512]{2,1,0:T(8,128)S(1)}, u32[]{:S(2)}, u32[]{:S(2)}) collective-permute-start(f32[4,16,512]{2,1,0:T(8,128)S(1)} %get-tuple-element.37), channel_id=1, source_target_pairs={{1,0},{2,1},{3,2},{4,3},{5,4},{6,5},{7,6},{8,7},{9,8},{10,9},{11,1... | collective-permute-start | bytes 393224 | tf_op jit(solution)/shard_map/ppermute | solution.py:695
  11.1 7.0 %inner_advance.1 = (bf16[4,96,512]{2,1,0:T(8,128)(2,1)}, bf16[4,96,512]{2,1,0:T(8,128)(2,1)}, bf16[4,96,512]{2,1,0:T(8,128)(2,1)}, bf16[4,96,512]{2,1,0:T(8,128)...) custom-call(f32[4,96,512]{2,1,0:T(8,128)} %heat.3, ...), custom_call_target="tpu_custom_call" | custom-call | flops 10000000000 | bytes 5000000 | tf_op jit(solution)/shard_map/inner_advance/pallas_call | solution.py:305
  18.1 0.0 collective-permute-done.low
  18.1 0.0 collective-permute-done.1.high
  18.1 5.2 %edge_advance.1 = (bf16[4,96,512]{2,1,0:T(8,128)(2,1)}, bf16[4,96,512]{2,1,0:T(8,128)(2,1)}, bf16[4,96,512]{2,1,0:T(8,128)(2,1)}, bf16[4,96,512]{2,1,0:T(8,128)(...) custom-call(f32[2,4,16,512]{3,2,1,0:T(8,128)S(1)} %get-tuple-element, ...), custom_call_target="tpu_custom_call", output_to_operand_aliasing={{0}: (10, {}), {1}: (11, {}), {2}: (12, {}), {3}: (13, {})} | custom-call | flops 10000000000 | bytes 5000000 | tf_op jit(solution)/shard_map/edge_advance/pallas_call | solution.py:554
  23.3 10.3 %all_to_all.5.sums = f32[16,8,128]{2,1,0:T(8,128)S(1)} all-to-all(f32[16,8,128]{2,1,0:T(8,128)S(1)} %get-tuple-element.46), channel_id=1, replica_groups=mesh['member'=2,'blk'=16] {'blk'}, dimensions={0} | all-to-all | bytes 131072 | tf_op jit(solution)/shard_map/all_to_all | solution.py:698
  33.6 4.2 %combine.1 = (f32[96,512]{1,0:T(8,128)}, f32[96,512]{1,0:T(8,128)}) custom-call(f32[16,8,128]{2,1,0:T(8,128)S(1)} %all_to_all.5.sums, f32[14,144,512]{2,1,0:T(8,128)S(1)} %get-tuple-element.47.fields), custom_call_target="tpu_custom_call" | custom-call | tf_op jit(solution)/shard_map/combine/pallas_call | solution.py:670
Async XLA Ops:
  0.6 0.7 %copy-start = (s32[1,8]{1,0:T(1,128)S(1)}, s32[1,8]{1,0:T(1,128)}, u32[]{:S(2)}) copy-start(s32[1,8]{1,0:T(1,128)} %flags.1) | copy-start | bytes 100
  1.3 0.7 %copy-start.1 = (f32[4]{0:T(128)S(1)}, f32[4]{0:T(128)}, u32[]{:S(2)}) copy-start(f32[4]{0:T(128)} %spacing.1) | copy-start | bytes 52
  5.5 12.6 %collective-permute-start = (f32[4,16,512]{2,1,0:T(8,128)S(1)}, f32[4,16,512]{2,1,0:T(8,128)S(1)}, u32[]{:S(2)}, u32[]{:S(2)}) collective-permute-start(f32[4,16,512]{2,1,0:T(8,128)S(1)} %get-tuple-element.36), channel_id=1, source_target_pairs={{0,1},{1,2},{2,3},{3,4},{4,5},{5,6},{6,7},{7,8},{8,9},{9,10},{10,1... | collective-permute-start | bytes 393224 | tf_op jit(solution)/shard_map/ppermute | solution.py:694
  6.1 12.0 %collective-permute-start.1 = (f32[4,16,512]{2,1,0:T(8,128)S(1)}, f32[4,16,512]{2,1,0:T(8,128)S(1)}, u32[]{:S(2)}, u32[]{:S(2)}) collective-permute-start(f32[4,16,512]{2,1,0:T(8,128)S(1)} %get-tuple-element.37), channel_id=1, source_target_pairs={{1,0},{2,1},{3,2},{4,3},{5,4},{6,5},{7,6},{8,7},{9,8},{10,9},{11,1... | collective-permute-start | bytes 393224 | tf_op jit(solution)/shard_map/ppermute | solution.py:695

commit v2 on v1

--- a/solution.py
+++ b/solution.py
@@ -15,9 +15,11 @@
 MARGIN = 8
 BASE = PAD + MARGIN
 KIB = 1024
+PARTS = 2
 VMEM_BYTES = 65472 * KIB
-PACK_ROOM = 10740 * KIB
-INNER_ROOM = 12660 * KIB
+FETCH_ROOM = 14480 * KIB
+PACK_ROOM = 32000 * KIB
+INNER_ROOM = 32000 * KIB
 EDGE_ROOM = 45 * KIB * KIB
 
 
@@ -60,7 +62,7 @@
 
 
 def upwind(speed, behind, ahead):
-    return jnp.where(speed > 0.0, speed * behind, speed * ahead)
+    return speed * jnp.where(speed > 0.0, behind, ahead)
 
 
 def face_speeds(u, v, east_wet, north_wet):
@@ -105,60 +107,88 @@
     return wet * (0.5 * (east_part + (north_of(cross) - south_of(cross))))
 
 
-def spacing_total(spacing):
-    total = spacing[0]
-    for k in range(1, spacing.shape[0]):
-        total = total + spacing[k]
-    return total
-
-
-def pack_kernel(
-    flags, spacing, heat, salt, u, v, damp, o_low, o_high, o_table, o_damp, windows, tips, sems
-):
-    levels, width, extent = u.shape
-    tiles = flags.shape[1]
-    messages = (o_high, o_low)
+class Band:
+    def __init__(self, parts):
+        self.parts = parts
+
+    def __getitem__(self, at):
+        return jnp.concatenate([part[at] for part in self.parts], axis=-1)
+
+
+def bands_of(refs):
+    return [Band(refs[q * PARTS : (q + 1) * PARTS]) for q in range(4)]
+
+
+def fetch_kernel(heat, salt, u, v, *refs):
+    width, extent = u.shape[1:]
+    parts, sems = refs[: 4 * PARTS], refs[4 * PARTS]
+    share = extent // PARTS
     copies = []
-    for end in range(2):
-        rows = pl.ds(0 if end == 0 else width - BASE, BASE)
-        into = pl.ds(MARGIN if end == 0 else 0, BASE)
-        tip = pl.ds(0 if end == 0 else width - MARGIN, MARGIN)
-        for src, dst in (
-            (u.at[:, rows], windows.at[0, end, :, into]),
-            (v.at[:, rows], windows.at[1, end, :, into]),
-            (heat.at[:, tip], tips.at[0, end]),
-            (salt.at[:, tip], tips.at[1, end]),
-        ):
-            copy = pltpu.make_async_copy(src, dst, sems.at[len(copies)])
+    for q, source in enumerate((heat, salt, u, v)):
+        for part in range(PARTS):
+            copy = pltpu.make_async_copy(
+                source.at[:, :, pl.ds(part * share, share)],
+                parts[q * PARTS + part].at[:, pl.ds(MARGIN, width)],
+                sems.at[len(copies)],
+            )
             copy.start()
             copies.append(copy)
-    copy = pltpu.make_async_copy(damp, o_damp, sems.at[len(copies)])
-    copy.start()
-    copies.append(copy)
+    for copy in copies:
+        copy.wait()
+
+
+def fetch(heat, salt, u, v):
+    levels, width, extent = u.shape
+    band = jax.ShapeDtypeStruct((levels, width + PAD, extent // PARTS), u.dtype)
+    return pl.pallas_call(
+        fetch_kernel,
+        out_shape=[band] * (4 * PARTS),
+        in_specs=[pl.BlockSpec(memory_space=pl.ANY)] * 4,
+        out_specs=[pl.BlockSpec(memory_space=pltpu.VMEM)] * (4 * PARTS),
+        scratch_shapes=[pltpu.SemaphoreType.DMA((4 * PARTS,))],
+        cost_estimate=pl.CostEstimate(
+            flops=10000000000, bytes_accessed=5000000, transcendentals=0
+        ),
+        compiler_params=pltpu.CompilerParams(vmem_limit_bytes=VMEM_BYTES - FETCH_ROOM),
+        name="fetch",
+    )(heat, salt, u, v)
+
+
+def pack_kernel(flags, spacing, damp, *refs):
+    heat, salt, u, v = bands_of(refs)
+    o_low, o_high, o_table = refs[4 * PARTS :]
+    levels = spacing.shape[1]
+    width, extent = damp.shape
+    tiles = flags.shape[1]
+    flows, tracers = (u, v), (heat, salt)
+    messages = (o_high, o_low)
     lane = lanes((MARGIN, extent))
     wet = jnp.zeros((MARGIN, extent), jnp.float32)
+    flag = flags[...].astype(jnp.float32)
     for tile in range(tiles):
         inside = (lane >= tile * (extent // tiles)) & (lane < (tile + 1) * (extent // tiles))
-        wet = jnp.where(inside, flags[0, tile].astype(jnp.float32), wet)
+        wet = jnp.where(inside, flag[:, tile : tile + 1], wet)
     o_table[0:MARGIN] = wet
     wet_row = wet[0:1]
     east_wet = wet_row * wet_row
     north_wet = north_wetness(wet)[0:1]
-    total = spacing_total(spacing)
     row = rows_in((MARGIN, extent))
+    thick = [spacing[:, k : k + 1] for k in range(levels)]
+    total = thick[0]
+    for k in range(1, levels):
+        total = total + thick[k]
     weights = jnp.zeros((MARGIN, extent), jnp.float32)
     for k in range(levels):
-        weights = jnp.where(row == k, spacing[k], weights)
+        weights = jnp.where(row == k, thick[k], weights)
     o_table[MARGIN:PAD] = weights / total
-    for copy in copies:
-        copy.wait()
     for end in range(2):
         message = messages[end]
-
-        def level_step(k, sums, end=end):
+        rows = slice(0, 2 * PAD) if end == 0 else slice(width - PAD, width + PAD)
+
+        def level_step(k, sums, rows=rows):
             weight = o_table[pl.ds(MARGIN + k, 1)]
-            qu = windows[0, end, k]
-            qv = windows[1, end, k]
+            qu = u[k, rows]
+            qv = v[k, rows]
             east, north = face_speeds(qu, qv, east_wet, north_wet)
             au = advect(qu, east, north, wet_row)
             av = advect(qv, east, north, wet_row)
@@ -168,21 +198,19 @@
         flow, cross = lax.fori_loop(0, levels, level_step, (zero, zero))
         message[0] = divergence(wet_row, flow, cross)
         first = 0 if end == 0 else width - PAD
-        message[1] = o_damp[first : first + PAD]
+        message[1] = damp[first : first + PAD]
+        tip = slice(MARGIN, PAD) if end == 0 else slice(width, width + MARGIN)
         for q in range(2):
             merged = jnp.zeros((MARGIN, extent), jnp.float32)
             for k in range(levels):
-                if end == 0:
-                    piece = shift(windows[q, 0, k, MARGIN:PAD], 2 * k, 0)
-                else:
-                    piece = shift(windows[q, 1, k, PAD:BASE], 2 * k + 2 - MARGIN, 0)
-                merged = jnp.where(row // 2 == k, piece, merged)
+                offset = 2 * k if end == 0 else 2 * k + 2 - MARGIN
+                merged = jnp.where(row // 2 == k, shift(flows[q][k, tip], offset, 0), merged)
             message[2, q * MARGIN : (q + 1) * MARGIN] = merged
         merged = jnp.zeros((MARGIN, extent), jnp.float32)
         for q in range(2):
             for k in range(levels):
                 place = q * levels + k
-                piece = shift(tips[q, end, k], place if end == 0 else place + 1, 0)
+                piece = shift(tracers[q][k, tip], place if end == 0 else place + 1, 0)
                 merged = jnp.where(row == place, piece, merged)
         message[3, 0:MARGIN] = merged
         if end == 0:
@@ -196,56 +224,26 @@
         )
 
 
-def pack(flags, spacing, heat, salt, u, v, damp):
-    levels, width, extent = u.shape
-    message = jax.ShapeDtypeStruct((4, PAD, extent), jnp.float32)
-    smem = pl.BlockSpec(memory_space=pltpu.SMEM)
+def pack(flags, spacing, damp, bands):
+    extent = damp.shape[1]
+    f32 = jnp.float32
+    message = jax.ShapeDtypeStruct((4, PAD, extent), f32)
+    vmem = pl.BlockSpec(memory_space=pltpu.VMEM)
     return pl.pallas_call(
         pack_kernel,
-        out_shape=[
-            message,
-            message,
-            jax.ShapeDtypeStruct((PAD, extent), jnp.float32),
-            jax.ShapeDtypeStruct(damp.shape, jnp.float32),
-        ],
-        in_specs=[smem, smem] + [pl.BlockSpec(memory_space=pl.ANY)] * 5,
-        out_specs=[pl.BlockSpec(memory_space=pltpu.VMEM)] * 4,
-        scratch_shapes=[
-            pltpu.VMEM((2, 2, levels, 2 * PAD, extent), jnp.float32),
-            pltpu.VMEM((2, 2, levels, MARGIN, extent), jnp.float32),
-            pltpu.SemaphoreType.DMA((9,)),
-        ],
+        out_shape=[message, message, jax.ShapeDtypeStruct((PAD, extent), f32)],
+        in_specs=[vmem] * (3 + len(bands)),
+        out_specs=[vmem] * 3,
         compiler_params=pltpu.CompilerParams(vmem_limit_bytes=VMEM_BYTES - PACK_ROOM),
         name="pack",
-    )(flags, spacing, heat, salt, u, v, damp)
-
-
-def inner_kernel(
-    heat, salt, u, v, table,
-    o_heat, o_salt, o_u, o_v, r_heat, r_salt, r_u, r_v, o_edge, o_start,
-    bands, staged, tu, tv, sems, out_sems,
-):
-    levels, width, extent = u.shape
-    sources = (heat, salt, u, v)
-    targets = (o_heat, o_salt, o_u, o_v)
-    rims = (r_heat, r_salt, r_u, r_v)
-    inside = width - 2 * PAD
-
-    def load(q, k):
-        return pltpu.make_async_copy(
-            sources[q].at[k], bands.at[q, k, pl.ds(MARGIN, width)], sems.at[q, k]
-        )
-
-    def store(q, k):
-        return pltpu.make_async_copy(
-            staged.at[q, k, pl.ds(PAD, inside)],
-            targets[q].at[k, pl.ds(PAD, inside)],
-            out_sems.at[q, k],
-        )
-
-    for k in range(levels):
-        for q in (2, 3, 0, 1):
-            load(q, k).start()
+    )(flags, spacing, damp, *bands)
+
+
+def inner_kernel(table, *refs):
+    heat, salt, u, v = bands_of(refs)
+    staged, o_start, tu, tv = refs[4 * PARTS :]
+    levels = staged.shape[1]
+    width, extent = o_start.shape
     wet = table[0:1]
     north_wet = north_wetness(table[0:MARGIN])[0:1]
     east_wet = wet * wet
@@ -254,15 +252,13 @@
 
     def level_step(k, carry):
         weight = table[pl.ds(MARGIN + k, 1)]
-        for q in (2, 3, 0, 1):
-            load(q, k).wait()
 
         def strip(index, carry):
             local = pl.ds(pl.multiple_of(index * PAD, PAD), PAD)
             later = pl.ds(pl.multiple_of(index * PAD + MARGIN, MARGIN), PAD)
             rows = pl.ds(pl.multiple_of(index * PAD, MARGIN), 2 * PAD)
-            qu = bands[2, k, rows]
-            qv = bands[3, k, rows]
+            qu = u[k, rows]
+            qv = v[k, rows]
             east, north = face_speeds(qu, qv, east_wet, north_wet)
             au = advect(qu, east, north, wet)
             av = advect(qv, east, north, wet)
@@ -270,17 +266,11 @@
             staged[3, k, local] = av.astype(staged.dtype)
             tu[later] += weight * au
             tv[later] += weight * av
-            staged[0, k, local] = advect(bands[0, k, rows], east, north, wet).astype(staged.dtype)
-            staged[1, k, local] = advect(bands[1, k, rows], east, north, wet).astype(staged.dtype)
+            staged[0, k, local] = advect(heat[k, rows], east, north, wet).astype(staged.dtype)
+            staged[1, k, local] = advect(salt[k, rows], east, north, wet).astype(staged.dtype)
             return carry
 
         lax.fori_loop(0, width // PAD, strip, 0)
-        for q in range(4):
-            store(q, k).start()
-            rims[q][0, k] = bands[q, k, MARGIN:BASE]
-            rims[q][1, k] = bands[q, k, width - MARGIN : width + MARGIN]
-            o_edge[q, 0, k] = staged[q, k, 0:PAD]
-            o_edge[q, 1, k] = staged[q, k, width - PAD : width]
         return carry
 
     lax.fori_loop(0, levels, level_step, 0)
@@ -290,50 +280,52 @@
         cross = tv[first + MARGIN : first + BASE]
         east_part = (shift(flow, -1, 0) - shift(flow, 1, 0))[MARGIN:BASE]
         o_start[keep] = wet * (0.5 * (east_part + (north_of(cross) - south_of(cross))))
-    for k in range(levels):
-        for q in range(4):
-            store(q, k).wait()
-
-
-def inner_advance(heat, salt, u, v, table):
-    levels, width, extent = u.shape
+
+
+def inner_advance(table, bands):
+    levels, padded, share = bands[0].shape
+    width, extent = padded - PAD, share * PARTS
     f32 = jnp.float32
-    tracer = jax.ShapeDtypeStruct(u.shape, jnp.bfloat16)
-    plane = jax.ShapeDtypeStruct((width, extent), f32)
     vmem = pl.BlockSpec(memory_space=pltpu.VMEM)
-    anywhere = pl.BlockSpec(memory_space=pl.ANY)
     return pl.pallas_call(
         inner_kernel,
-        out_shape=[tracer] * 4
-        + [jax.ShapeDtypeStruct((2, levels, PAD, extent), f32)] * 4
-        + [jax.ShapeDtypeStruct((4, 2, levels, PAD, extent), jnp.bfloat16), plane],
-        in_specs=[anywhere] * 4 + [vmem],
-        out_specs=[anywhere] * 4 + [vmem] * 6,
+        out_shape=[
+            jax.ShapeDtypeStruct((4, levels, width, extent), jnp.bfloat16),
+            jax.ShapeDtypeStruct((width, extent), f32),
+        ],
+        in_specs=[vmem] * (1 + len(bands)),
+        out_specs=[vmem] * 2,
         scratch_shapes=[
-            pltpu.VMEM((4, levels, width + PAD, extent), f32),
-            pltpu.VMEM((4, levels, width, extent), jnp.bfloat16),
             pltpu.VMEM((width + PAD, extent), f32),
             pltpu.VMEM((width + PAD, extent), f32),
-            pltpu.SemaphoreType.DMA((4, levels)),
-            pltpu.SemaphoreType.DMA((4, levels)),
         ],
         cost_estimate=pl.CostEstimate(
             flops=10000000000, bytes_accessed=5000000, transcendentals=0
         ),
         compiler_params=pltpu.CompilerParams(vmem_limit_bytes=VMEM_BYTES - INNER_ROOM),
         name="inner_advance",
-    )(heat, salt, u, v, table)
-
-
-def edge_kernel(
-    r_heat, r_salt, r_u, r_v, edge_in, start_in, damp, table, low, high, i_heat, i_salt, i_u, i_v,
-    o_heat, o_salt, o_u, o_v, fields, o_sums,
-    ocean, diag, edge_out, acc, out_sems,
-):
-    rims = (r_heat, r_salt, r_u, r_v)
-    levels, extent = r_u.shape[1], r_u.shape[3]
-    width = start_in.shape[0]
+    )(table, *bands)
+
+
+def edge_kernel(staged, start_in, damp, table, low, high, *refs):
+    heat, salt, u, v = bands_of(refs)
+    refs = refs[4 * PARTS :]
+    levels = staged.shape[1]
+    width, extent = start_in.shape
     span = width + 2 * BASE
+    flows, tracers = (u, v), (heat, salt)
+    o_heat, o_salt, o_u, o_v, fields, o_sums = refs[:6]
+    ocean, diag, even, odd, edge_out, acc, out_sems = refs[6:]
+    masked = (even, odd)
+    targets = (o_heat, o_salt, o_u, o_v)
+    inside = pl.ds(PAD, width - 2 * PAD)
+    results = []
+    for q in range(4):
+        copy = pltpu.make_async_copy(
+            staged.at[q, :, inside], targets[q].at[:, inside], out_sems.at[8 + q]
+        )
+        copy.start()
+        results.append(copy)
     wet8 = table[0:MARGIN]
     row = rows_in((MARGIN, extent))
     for block in range(BASE // MARGIN, (BASE + width) // MARGIN):
@@ -364,16 +356,19 @@
         north_own = north_wetness(wet8)
         north_out = north_wetness(wet_out)
 
+        mine_at = slice(MARGIN, BASE) if side == 0 else slice(width - MARGIN, width + MARGIN)
+        rim_at = slice(0, PAD) if side == 0 else slice(width - PAD, width)
+
         def level_step(k, sums, side=side, message=message, east_own=east_own,
                        east_out=east_out, north_own=north_own, north_out=north_out,
-                       wet_out=wet_out):
+                       wet_out=wet_out, mine_at=mine_at, rim_at=rim_at):
             weight = table[pl.ds(MARGIN + k, 1)]
             own, out = [], []
             for q in (2, 3):
                 pair = message[2, (q - 2) * MARGIN : (q - 1) * MARGIN]
-                mine = rims[q][side, k]
+                mine = flows[q - 2][k, mine_at]
                 if side == 0:
-                    piece = pltpu.roll(pair, MARGIN - 2 - 2 * k, 0)
+                    piece = pltpu.roll(pair, (2 * MARGIN - 2 - 2 * k) % MARGIN, 0)
                     own.append(jnp.concatenate([piece, mine], axis=0))
                     out.append(jnp.concatenate([piece, piece, mine[:MARGIN]], axis=0))
                 else:
@@ -385,7 +380,7 @@
             av = advect(own[1], east, north, wet8)
             fresh = [None, None, au, av]
             for q in range(2):
-                mine = rims[q][side, k]
+                mine = tracers[q][k, mine_at]
                 single = message[3, 0:MARGIN]
                 place = q * levels + k
                 if side == 0:
@@ -396,7 +391,7 @@
                     window = jnp.concatenate([mine, piece], axis=0)
                 fresh[q] = advect(window, east, north, wet8)
             for q in range(4):
-                old = edge_in[q, side, k].astype(jnp.float32)
+                old = staged[q, k, rim_at].astype(jnp.float32)
                 if side == 0:
                     value = jnp.concatenate([fresh[q], old[MARGIN:]], axis=0)
                 else:
@@ -448,8 +443,7 @@
             fields[1, top : top + MARGIN] = jnp.where(row < 2, whole[MARGIN:], given[:MARGIN])
             fields[1, top + MARGIN : top + PAD] = given[MARGIN:]
 
-    results = []
-    for q, target in enumerate((o_heat, o_salt, o_u, o_v)):
+    for q, target in enumerate(targets):
         for side in range(2):
             first = 0 if side == 0 else width - PAD
             copy = pltpu.make_async_copy(
@@ -475,6 +469,7 @@
     square = (none, none)
     for strip in range(strips):
         keep = slice(MARGIN + strip * PAD, BASE + strip * PAD)
+        masked[0][keep] = (0.5 * ocean[keep]) * fields[1, keep]
         fields[0, keep] = jnp.zeros((PAD, extent), jnp.float32)
         if 0 < strip < strips - 1:
             value = fields[1, keep]
@@ -485,22 +480,24 @@
         acc[0, slot * MARGIN : (slot + 1) * MARGIN] = none
         acc[1, slot * MARGIN : (slot + 1) * MARGIN] = none
 
-    def basis_step(j, carry):
-        scale = jnp.where(j == 0, 0.5, 1.0)
+    def basis_step(j, now, scale):
         mixed, square = (none, none), (none, none)
         for strip in range(strips):
             start = MARGIN + strip * PAD
             around = slice(start - MARGIN, start + BASE)
             keep = slice(start, start + PAD)
-            wide = fields[j + 1, around]
-            masked = wide * ocean[around]
-            sides = (shift(masked, -1, 0) + shift(masked, 1, 0))[MARGIN:BASE]
-            column = masked[MARGIN:BASE] + 0.5 * sides
+            wide = masked[now][around]
+            sides = (shift(wide, -1, 0) + shift(wide, 1, 0))[MARGIN:BASE]
+            column = wide[MARGIN:BASE] + 0.5 * sides
             near = sides + (north_of(column) + south_of(column))
-            centre = wide[MARGIN:BASE]
-            image = diag[keep] * centre - (0.5 * ocean[keep]) * near
-            following = scale * image - fields[j, keep]
+            centre = fields[j + 1, keep]
+            wet = ocean[keep]
+            following = diag[keep] * centre - wet * near
+            if scale is not None:
+                following = scale * following
+            following = following - fields[j, keep]
             fields[j + 2, keep] = following
+            masked[1 - now][keep] = (0.5 * wet) * following
             if 0 < strip < strips - 1:
                 mixed = inner(centre, following, mixed)
                 square = inner(following, following, square)
@@ -508,9 +505,13 @@
             at = pl.ds(pl.multiple_of(place * MARGIN, MARGIN), MARGIN)
             acc[0, at] = value[0]
             acc[1, at] = value[1]
+
+    def step_pair(index, carry):
+        basis_step(2 * index, 0, jnp.where(index == 0, 0.5, 1.0))
+        basis_step(2 * index + 1, 1, None)
         return carry
 
-    lax.fori_loop(0, STEPS, basis_step, 0)
+    lax.fori_loop(0, STEPS // 2, step_pair, 0)
 
     slots = acc.shape[1] // MARGIN
     pairs = [
@@ -542,14 +543,13 @@
         copy.wait()
 
 
-def edge_advance(damp, table, low, high, inner, members):
-    *tracers, r_heat, r_salt, r_u, r_v, edge, start = inner
-    levels, width, extent = tracers[0].shape
+def edge_advance(staged, start, damp, table, low, high, bands, members):
+    levels, width, extent = staged.shape[1:]
     span = width + 2 * BASE
     slots = 32
     anywhere = pl.BlockSpec(memory_space=pl.ANY)
     vmem = pl.BlockSpec(memory_space=pltpu.VMEM)
-    tracer = jax.ShapeDtypeStruct(tracers[0].shape, jnp.bfloat16)
+    tracer = jax.ShapeDtypeStruct((levels, width, extent), staged.dtype)
     f32 = jnp.float32
     return pl.pallas_call(
         edge_kernel,
@@ -558,22 +558,23 @@
             jax.ShapeDtypeStruct((STEPS + 2, span, extent), f32),
             jax.ShapeDtypeStruct((members, MARGIN, 128), f32),
         ],
-        in_specs=[vmem] * 10 + [anywhere] * 4,
+        in_specs=[vmem] * (6 + len(bands)),
         out_specs=[anywhere] * 4 + [vmem] * 2,
         scratch_shapes=[
             pltpu.VMEM((span, extent), f32),
             pltpu.VMEM((span, extent), f32),
+            pltpu.VMEM((span, extent), f32),
+            pltpu.VMEM((span, extent), f32),
             pltpu.VMEM((4, 2, levels, PAD, extent), jnp.bfloat16),
             pltpu.VMEM((2, slots * MARGIN, 128), f32),
-            pltpu.SemaphoreType.DMA((8,)),
+            pltpu.SemaphoreType.DMA((12,)),
         ],
-        input_output_aliases={10 + q: q for q in range(4)},
         cost_estimate=pl.CostEstimate(
             flops=10000000000, bytes_accessed=5000000, transcendentals=0
         ),
         compiler_params=pltpu.CompilerParams(vmem_limit_bytes=VMEM_BYTES - EDGE_ROOM),
         name="edge_advance",
-    )(r_heat, r_salt, r_u, r_v, edge, start, damp, table, low, high, *tracers)
+    )(staged, start, damp, table, low, high, *bands)
 
 
 def combine_kernel(sums, fields, height, resid):
@@ -631,19 +632,32 @@
     zero = jnp.zeros_like(unit)
     r_products, p_products = moments, moments
     c_r, c_p, c_x = (unit, zero), (unit, zero), zero
+
+    def pick(x, k):
+        return at(x[0], k), at(x[1], k)
+
+    def quarter_sum(before, here, after):
+        out = pair_add(pair_add(after, before), (2.0 * here[0], 2.0 * here[1]))
+        return 0.25 * out[0], 0.25 * out[1]
+
+    norm = pick(r_products, 0)
     for k in range(STEPS):
-        image = image_of_products(p_products)
-        norm_now = at(r_products[0], k)
-        alpha = norm_now / at(image[0], k)
-        change = pair_scale(image, -alpha)
-        r_products = pair_add(r_products, change)
+        near = [pick(p_products, abs(k - 1)), pick(p_products, k)]
+        near += [pick(p_products, k + 1), pick(p_products, k + 2)]
+        energy = quarter_sum(near[0], near[1], near[2])
+        alpha = norm[0] / energy[0]
         c_x = c_x + alpha * c_p[0]
         c_r = pair_add(c_r, pair_scale(image_of_coefficients(c_p), -alpha))
         if k + 1 < STEPS:
+            change = pair_scale(image_of_products(p_products), -alpha)
+            following = pair_scale(quarter_sum(near[1], near[2], near[3]), -alpha)
+            following = pair_add(pick(r_products, k + 1), following)
+            r_products = pair_add(r_products, change)
             lead = 0.5 if k == 0 else 0.25
-            beta = (-lead * alpha) * at(r_products[0], k + 1) / norm_now
+            beta = (-lead * alpha) * following[0] / norm[0]
             p_products = pair_add(r_products, pair_scale(p_products, beta))
             c_p = pair_add(c_r, pair_scale(c_p, beta))
+            norm = following
 
     width = height.shape[0]
     weights_x = [at(c_x, j)[0:1] for j in range(STEPS + 1)]
@@ -653,13 +667,11 @@
         wide = slice(BASE + first, BASE + first + MARGIN)
         for left in range(0, height.shape[1], 128):
             cols = slice(left, left + 128)
-            h = None
-            for j in range(STEPS + 1):
+            value = fields[1, wide, cols]
+            h, r = weights_x[0] * value, weights_r[0] * value
+            for j in range(1, STEPS + 1):
                 value = fields[j + 1, wide, cols]
-                if h is None:
-                    h, r = weights_x[0] * value, weights_r[0] * value
-                else:
-                    h, r = h + weights_x[j] * value, r + weights_r[j] * value
+                h, r = h + weights_x[j] * value, r + weights_r[j] * value
             height[keep, cols] = h
             resid[keep, cols] = r
 
@@ -687,14 +699,16 @@
     water_tile_flags,
 ):
     members = lax.axis_size("blk")
-    fields = (heat_anomaly, saltiness_anomaly, first_axis_flow, second_axis_flow)
-    to_next, to_last, table, damp = pack(water_tile_flags, layer_spacing, *fields, diagonal_shift)
+    bands = fetch(heat_anomaly, saltiness_anomaly, first_axis_flow, second_axis_flow)
+    to_next, to_last, table = pack(water_tile_flags, layer_spacing[None], diagonal_shift, bands)
     forward = [(i, (i + 1) % members) for i in range(members)]
     backward = [(target, source) for source, target in forward]
     low = lax.ppermute(to_next, "blk", forward)
     high = lax.ppermute(to_last, "blk", backward)
-    inner = inner_advance(*fields, table)
-    *tracers, basis, sums = edge_advance(damp, table, low, high, inner, members)
+    staged, start = inner_advance(table, bands)
+    *tracers, basis, sums = edge_advance(
+        staged, start, diagonal_shift, table, low, high, bands, members
+    )
     gathered = lax.all_to_all(sums, "blk", 0, 0)
     height, resid = combine(gathered, basis, diagonal_shift.shape[0])
     return (*tracers, height, resid)

time: 38.1 us -> 33.2 us (0.87)
  Pallas kernels: 20 us -> 16.4 us
  local copies, waits for them, and re-layouts: 1.3 us -> 0.01 us
    pallas_call x1, Pallas kernels: 3.56 us -> 1.74 us  [pack(): pl.pallas_call(pack_kernel, out_shape=[message, message, jax.ShapeDtypeSt...]
    pallas_call x1, Pallas kernels: 4.23 us -> 2.74 us  [combine(): pl.pallas_call(combine_kernel, out_shape=[plane, plane], in_specs=[vmem,...]
    unnamed x4 -> x6, local copies, waits for them, and re-layouts: 1.3 us -> 0.01 us
    pallas_call x1 -> x2, Pallas kernels: 6.99 us -> 6.91 us  [the longest x1 4.94 us: inner_advance(): pl.pallas_call(inner_kernel, out_shape=[jax.ShapeDtypeStruct((4, levels,...]
  transfers between devices with their start and end apart: 2 -> 2, of which waited for: 0 -> 0; matrix products, arithmetic and copies ran while one was open for 0% -> 0% of each run, Pallas kernels for 18% -> 15%
where the time goes in v2:
time: 33.2 us; the launch traced here: 33.1 us
  Pallas kernels  16.4 us (49%)
  blocking collectives  10.3 us (31%)
  starting transfers between devices  5.56 us (17%)
  between operations  0.73 us (2%)
    all_to_all x1, blocking collectives, on_device(): gathered = lax.all_to_all(sums, 'blk', 0, 0)  10.3 us
    pallas_call x1, Pallas kernels, edge_advance(): pl.pallas_call(edge_kernel, out_shape=[tracer] * 4 + [jax.ShapeDtypeStruc...  5.04 us
    ppermute x1, starting transfers between devices, on_device(): high = lax.ppermute(to_last, 'blk', backward)  5.02 us
    pallas_call x1, Pallas kernels, inner_advance(): pl.pallas_call(inner_kernel, out_shape=[jax.ShapeDtypeStruct((4, levels,...  4.94 us
    pallas_call x1, Pallas kernels, combine(): pl.pallas_call(combine_kernel, out_shape=[plane, plane], in_specs=[vmem,...  2.74 us
    pallas_call x1, Pallas kernels, fetch(): pl.pallas_call(fetch_kernel, out_shape=[band] * (4 * PARTS), in_specs=[pl...  1.98 us
    pallas_call x1, Pallas kernels, pack(): pl.pallas_call(pack_kernel, out_shape=[message, message, jax.ShapeDtypeSt...  1.74 us
  transfers between devices with their start and end apart: 2, of which 0 were waited for; matrix products, arithmetic and copies ran while one was open for 0% of the time, Pallas kernels for 15%

profile of v2, /device:TPU:0, one launch (start us, length us, event | category | flops | bytes accessed | tf_op | source)
XLA Modules:
  0.0 33.1 jit_solution(8091283504342969732)
XLA Ops:
  0.6 0.0 copy-start
  0.6 0.0 copy-start.1
  0.7 0.0 copy-start.2
  0.7 2.0 %fetch.1 = (f32[4,112,256]{2,1,0:T(8,128)S(1)}, f32[4,112,256]{2,1,0:T(8,128)S(1)}, f32[4,112,256]{2,1,0:T(8,128)S(1)}, f32[4,112,256]{2,1,0:T(8,128)S(1)}, f32[...) custom-call(f32[4,96,512]{2,1,0:T(8,128)} %heat.1, ...), custom_call_target="tpu_custom_call" | custom-call | flops 10000000000 | bytes 5000000 | tf_op jit(solution)/shard_map/fetch/pallas_call | solution.py:143
  2.6 0.0 copy-done
  2.7 0.0 copy-done.1
  2.7 0.0 copy-done.2
  2.7 1.7 %pack.1 = (f32[4,16,512]{2,1,0:T(8,128)S(1)}, f32[4,16,512]{2,1,0:T(8,128)S(1)}, f32[16,512]{1,0:T(8,128)S(1)}) custom-call(s32[1,8]{1,0:T(1,128)S(1)} %copy-done.1, f32[1,4]{1,0:T(1,128)S(1)} %bitcast.1, f32[96,512]{1,0:T(8,128)S(1)} %copy-done, f32[4,112,256]{2,1,0:T(8,128)S(1)} %get-tuple-element.27.refs_0_, ...), custom_call_target="tpu_custom_call" | custom-call | tf_op jit(solution)/shard_map/pack/pallas_call | solution.py:232
  4.4 0.5 %collective-permute-start = (f32[4,16,512]{2,1,0:T(8,128)S(1)}, f32[4,16,512]{2,1,0:T(8,128)S(1)}, u32[]{:S(2)}, u32[]{:S(2)}) collective-permute-start(f32[4,16,512]{2,1,0:T(8,128)S(1)} %get-tuple-element.38), channel_id=1, source_target_pairs={{0,1},{1,2},{2,3},{3,4},{4,5},{5,6},{6,7},{7,8},{8,9},{9,10},{10,1... | collective-permute-start | bytes 393224 | tf_op jit(solution)/shard_map/ppermute | solution.py:706
  5.0 5.0 %collective-permute-start.1 = (f32[4,16,512]{2,1,0:T(8,128)S(1)}, f32[4,16,512]{2,1,0:T(8,128)S(1)}, u32[]{:S(2)}, u32[]{:S(2)}) collective-permute-start(f32[4,16,512]{2,1,0:T(8,128)S(1)} %get-tuple-element.39), channel_id=1, source_target_pairs={{1,0},{2,1},{3,2},{4,3},{5,4},{6,5},{7,6},{8,7},{9,8},{10,9},{11,1... | collective-permute-start | bytes 393224 | tf_op jit(solution)/shard_map/ppermute | solution.py:707
  10.0 4.9 %inner_advance.1 = (bf16[4,4,96,512]{3,2,1,0:T(8,128)(2,1)S(1)}, f32[96,512]{1,0:T(8,128)S(1)}) custom-call(f32[16,512]{1,0:T(8,128)S(1)} %get-tuple-element.35.table, f32[4,112,256]{2,1,0:T(8,128)S(1)} %get-tuple-element.27.refs_0_, f32[4,112,256]{2,1,0:T(8,128)S(1)} %get-tuple-element.28.refs_1_, f32[4,112,256]{2,1,0:T(8,128)S(1)} %get-tuple-element.29.refs_2_, ...), custom_call_target="tpu_custom_call" | custom-call | flops 10000000000 | bytes 5000000 | tf_op jit(solution)/shard_map/inner_advance/pallas_call | solution.py:290
  14.9 0.0 collective-permute-done.low
  14.9 0.0 collective-permute-done.1.high
  15.0 5.0 %edge_advance.1 = (bf16[4,96,512]{2,1,0:T(8,128)(2,1)}, bf16[4,96,512]{2,1,0:T(8,128)(2,1)}, bf16[4,96,512]{2,1,0:T(8,128)(2,1)}, bf16[4,96,512]{2,1,0:T(8,128)(...) custom-call(bf16[4,4,96,512]{3,2,1,0:T(8,128)(2,1)S(1)} %get-tuple-element.36.staged, ...), custom_call_target="tpu_custom_call" | custom-call | flops 10000000000 | bytes 5000000 | tf_op jit(solution)/shard_map/edge_advance/pallas_call | solution.py:554
  20.0 10.3 %all_to_all.5.sums = f32[16,8,128]{2,1,0:T(8,128)S(1)} all-to-all(f32[16,8,128]{2,1,0:T(8,128)S(1)} %get-tuple-element.44), channel_id=1, replica_groups=mesh['member'=2,'blk'=16] {'blk'}, dimensions={0} | all-to-all | bytes 131072 | tf_op jit(solution)/shard_map/all_to_all | solution.py:712
  30.3 2.7 %combine.1 = (f32[96,512]{1,0:T(8,128)}, f32[96,512]{1,0:T(8,128)}) custom-call(f32[16,8,128]{2,1,0:T(8,128)S(1)} %all_to_all.5.sums, f32[14,144,512]{2,1,0:T(8,128)S(1)} %get-tuple-element.45.fields), custom_call_target="tpu_custom_call" | custom-call | tf_op jit(solution)/shard_map/combine/pallas_call | solution.py:682
Async XLA Ops:
  0.6 2.0 %copy-start = (f32[96,512]{1,0:T(8,128)S(1)}, f32[96,512]{1,0:T(8,128)}, u32[]{:S(2)}) copy-start(f32[96,512]{1,0:T(8,128)} %damp.3) | copy-start | bytes 589828
  0.6 2.0 %copy-start.1 = (s32[1,8]{1,0:T(1,128)S(1)}, s32[1,8]{1,0:T(1,128)}, u32[]{:S(2)}) copy-start(s32[1,8]{1,0:T(1,128)} %flags.1) | copy-start | bytes 100
  0.7 2.0 %copy-start.2 = (f32[4]{0:T(128)S(1)}, f32[4]{0:T(128)}, u32[]{:S(2)}) copy-start(f32[4]{0:T(128)} %param.11) | copy-start | bytes 52
  4.4 10.5 %collective-permute-start = (f32[4,16,512]{2,1,0:T(8,128)S(1)}, f32[4,16,512]{2,1,0:T(8,128)S(1)}, u32[]{:S(2)}, u32[]{:S(2)}) collective-permute-start(f32[4,16,512]{2,1,0:T(8,128)S(1)} %get-tuple-element.38), channel_id=1, source_target_pairs={{0,1},{1,2},{2,3},{3,4},{4,5},{5,6},{6,7},{7,8},{8,9},{9,10},{10,1... | collective-permute-start | bytes 393224 | tf_op jit(solution)/shard_map/ppermute | solution.py:706
  5.0 10.0 %collective-permute-start.1 = (f32[4,16,512]{2,1,0:T(8,128)S(1)}, f32[4,16,512]{2,1,0:T(8,128)S(1)}, u32[]{:S(2)}, u32[]{:S(2)}) collective-permute-start(f32[4,16,512]{2,1,0:T(8,128)S(1)} %get-tuple-element.39), channel_id=1, source_target_pairs={{1,0},{2,1},{3,2},{4,3},{5,4},{6,5},{7,6},{8,7},{9,8},{10,9},{11,1... | collective-permute-start | bytes 393224 | tf_op jit(solution)/shard_map/ppermute | solution.py:707

commit v3 on v2

--- a/solution.py
+++ b/solution.py
@@ -195,7 +195,7 @@
             return sums[0] + weight * au, sums[1] + weight * av
 
         zero = jnp.zeros((PAD, extent), jnp.float32)
-        flow, cross = lax.fori_loop(0, levels, level_step, (zero, zero))
+        flow, cross = lax.fori_loop(0, levels, level_step, (zero, zero), unroll=4)
         message[0] = divergence(wet_row, flow, cross)
         first = 0 if end == 0 else width - PAD
         message[1] = damp[first : first + PAD]
@@ -270,7 +270,7 @@
             staged[1, k, local] = advect(salt[k, rows], east, north, wet).astype(staged.dtype)
             return carry
 
-        lax.fori_loop(0, width // PAD, strip, 0)
+        lax.fori_loop(0, width // PAD, strip, 0, unroll=2)
         return carry
 
     lax.fori_loop(0, levels, level_step, 0)
@@ -315,7 +315,7 @@
     span = width + 2 * BASE
     flows, tracers = (u, v), (heat, salt)
     o_heat, o_salt, o_u, o_v, fields, o_sums = refs[:6]
-    ocean, diag, even, odd, edge_out, acc, out_sems = refs[6:]
+    ocean, half, diag, even, odd, edge_out, acc, out_sems = refs[6:]
     masked = (even, odd)
     targets = (o_heat, o_salt, o_u, o_v)
     inside = pl.ds(PAD, width - 2 * PAD)
@@ -365,14 +365,15 @@
             weight = table[pl.ds(MARGIN + k, 1)]
             own, out = [], []
             for q in (2, 3):
-                pair = message[2, (q - 2) * MARGIN : (q - 1) * MARGIN]
+                place = (q - 2) * MARGIN + 2 * k
+                nearer, farther = message[2, pl.ds(place, 1)], message[2, pl.ds(place + 1, 1)]
                 mine = flows[q - 2][k, mine_at]
                 if side == 0:
-                    piece = pltpu.roll(pair, (2 * MARGIN - 2 - 2 * k) % MARGIN, 0)
+                    piece = jnp.where(row == MARGIN - 1, farther, nearer)
                     own.append(jnp.concatenate([piece, mine], axis=0))
                     out.append(jnp.concatenate([piece, piece, mine[:MARGIN]], axis=0))
                 else:
-                    piece = pltpu.roll(pair, (MARGIN - 2 * k) % MARGIN, 0)
+                    piece = jnp.where(row == 0, nearer, farther)
                     own.append(jnp.concatenate([mine, piece], axis=0))
                     out.append(jnp.concatenate([mine[MARGIN:], piece, piece], axis=0))
             east, north = face_speeds(own[0], own[1], east_own, north_own)
@@ -381,13 +382,12 @@
             fresh = [None, None, au, av]
             for q in range(2):
                 mine = tracers[q][k, mine_at]
-                single = message[3, 0:MARGIN]
-                place = q * levels + k
+                piece = jnp.broadcast_to(
+                    message[3, pl.ds(q * levels + k, 1)], (MARGIN, extent)
+                )
                 if side == 0:
-                    piece = pltpu.roll(single, (2 * MARGIN - 1 - place) % MARGIN, 0)
                     window = jnp.concatenate([piece, mine], axis=0)
                 else:
-                    piece = pltpu.roll(single, (MARGIN - place) % MARGIN, 0)
                     window = jnp.concatenate([mine, piece], axis=0)
                 fresh[q] = advect(window, east, north, wet8)
             for q in range(4):
@@ -409,7 +409,7 @@
 
         zero = jnp.zeros((MARGIN, extent), jnp.float32)
         flow, cross, flow_out, cross_out = lax.fori_loop(
-            0, levels, level_step, (zero, zero, zero, zero)
+            0, levels, level_step, (zero, zero, zero, zero), unroll=2
         )
         known = message[3, MARGIN:PAD]
         given = message[0]
@@ -469,7 +469,8 @@
     square = (none, none)
     for strip in range(strips):
         keep = slice(MARGIN + strip * PAD, BASE + strip * PAD)
-        masked[0][keep] = (0.5 * ocean[keep]) * fields[1, keep]
+        half[keep] = 0.5 * ocean[keep]
+        masked[0][keep] = half[keep] * fields[1, keep]
         fields[0, keep] = jnp.zeros((PAD, extent), jnp.float32)
         if 0 < strip < strips - 1:
             value = fields[1, keep]
@@ -491,13 +492,12 @@
             column = wide[MARGIN:BASE] + 0.5 * sides
             near = sides + (north_of(column) + south_of(column))
             centre = fields[j + 1, keep]
-            wet = ocean[keep]
-            following = diag[keep] * centre - wet * near
+            following = diag[keep] * centre - ocean[keep] * near
             if scale is not None:
                 following = scale * following
             following = following - fields[j, keep]
             fields[j + 2, keep] = following
-            masked[1 - now][keep] = (0.5 * wet) * following
+            masked[1 - now][keep] = half[keep] * following
             if 0 < strip < strips - 1:
                 mixed = inner(centre, following, mixed)
                 square = inner(following, following, square)
@@ -561,6 +561,7 @@
         in_specs=[vmem] * (6 + len(bands)),
         out_specs=[anywhere] * 4 + [vmem] * 2,
         scratch_shapes=[
+            pltpu.VMEM((span, extent), f32),
             pltpu.VMEM((span, extent), f32),
             pltpu.VMEM((span, extent), f32),
             pltpu.VMEM((span, extent), f32),

time: 33.2 us -> 31.5 us (0.949)
  Pallas kernels: 16.4 us -> 13.5 us
  blocking collectives: 10.3 us -> 11.5 us
    pallas_call x1, Pallas kernels: 4.94 us -> 3.62 us  [inner_advance(): pl.pallas_call(inner_kernel, out_shape=[jax.ShapeDtypeStruct((4, levels,...]
    all_to_all x1, blocking collectives: 10.3 us -> 11.5 us  [on_device(): gathered = lax.all_to_all(sums, 'blk', 0, 0)]
    pallas_call x1, Pallas kernels: 1.74 us -> 0.66 us  [pack(): pl.pallas_call(pack_kernel, out_shape=[message, message, jax.ShapeDtypeSt...]
    pallas_call x1, Pallas kernels: 5.04 us -> 4.49 us  [edge_advance(): pl.pallas_call(edge_kernel, out_shape=[tracer] * 4 + [jax.ShapeDtypeStruc...]
  transfers between devices with their start and end apart: 2 -> 2, of which waited for: 0 -> 0; matrix products, arithmetic and copies ran while one was open for 0% -> 0% of each run, Pallas kernels for 15% -> 12%
where the time goes in v3:
time: 31.5 us; the launch traced here: 31.3 us
  Pallas kernels  13.5 us (43%)
  blocking collectives  11.5 us (37%)
  starting transfers between devices  5.56 us (18%)
  between operations  0.73 us (2%)
    all_to_all x1, blocking collectives, on_device(): gathered = lax.all_to_all(sums, 'blk', 0, 0)  11.5 us
    ppermute x1, starting transfers between devices, on_device(): high = lax.ppermute(to_last, 'blk', backward)  5.02 us
    pallas_call x1, Pallas kernels, edge_advance(): pl.pallas_call(edge_kernel, out_shape=[tracer] * 4 + [jax.ShapeDtypeStruc...  4.49 us
    pallas_call x1, Pallas kernels, inner_advance(): pl.pallas_call(inner_kernel, out_shape=[jax.ShapeDtypeStruct((4, levels,...  3.62 us
    pallas_call x1, Pallas kernels, combine(): pl.pallas_call(combine_kernel, out_shape=[plane, plane], in_specs=[vmem,...  2.74 us
    pallas_call x1, Pallas kernels, fetch(): pl.pallas_call(fetch_kernel, out_shape=[band] * (4 * PARTS), in_specs=[pl...  1.98 us
    pallas_call x1, Pallas kernels, pack(): pl.pallas_call(pack_kernel, out_shape=[message, message, jax.ShapeDtypeSt...  0.66 us
  transfers between devices with their start and end apart: 2, of which 0 were waited for; matrix products, arithmetic and copies ran while one was open for 0% of the time, Pallas kernels for 12%

profile of v3, /device:TPU:0, one launch (start us, length us, event | category | flops | bytes accessed | tf_op | source)
XLA Modules:
  0.0 31.3 jit_solution(155728532196606169)
XLA Ops:
  0.6 0.0 copy-start
  0.6 0.0 copy-start.1
  0.7 0.0 copy-start.2
  0.7 2.0 %fetch.1 = (f32[4,112,256]{2,1,0:T(8,128)S(1)}, f32[4,112,256]{2,1,0:T(8,128)S(1)}, f32[4,112,256]{2,1,0:T(8,128)S(1)}, f32[4,112,256]{2,1,0:T(8,128)S(1)}, f32[...) custom-call(f32[4,96,512]{2,1,0:T(8,128)} %heat.1, ...), custom_call_target="tpu_custom_call" | custom-call | flops 10000000000 | bytes 5000000 | tf_op jit(solution)/shard_map/fetch/pallas_call | solution.py:143
  2.6 0.0 copy-done
  2.7 0.0 copy-done.1
  2.7 0.0 copy-done.2
  2.7 0.7 %pack.1 = (f32[4,16,512]{2,1,0:T(8,128)S(1)}, f32[4,16,512]{2,1,0:T(8,128)S(1)}, f32[16,512]{1,0:T(8,128)S(1)}) custom-call(s32[1,8]{1,0:T(1,128)S(1)} %copy-done.1, f32[1,4]{1,0:T(1,128)S(1)} %bitcast.1, f32[96,512]{1,0:T(8,128)S(1)} %copy-done, f32[4,112,256]{2,1,0:T(8,128)S(1)} %get-tuple-element.27.refs_0_, ...), custom_call_target="tpu_custom_call" | custom-call | tf_op jit(solution)/shard_map/pack/pallas_call | solution.py:232
  3.3 0.5 %collective-permute-start = (f32[4,16,512]{2,1,0:T(8,128)S(1)}, f32[4,16,512]{2,1,0:T(8,128)S(1)}, u32[]{:S(2)}, u32[]{:S(2)}) collective-permute-start(f32[4,16,512]{2,1,0:T(8,128)S(1)} %get-tuple-element.38), channel_id=1, source_target_pairs={{0,1},{1,2},{2,3},{3,4},{4,5},{5,6},{6,7},{7,8},{8,9},{9,10},{10,1... | collective-permute-start | bytes 393224 | tf_op jit(solution)/shard_map/ppermute | solution.py:707
  3.9 5.0 %collective-permute-start.1 = (f32[4,16,512]{2,1,0:T(8,128)S(1)}, f32[4,16,512]{2,1,0:T(8,128)S(1)}, u32[]{:S(2)}, u32[]{:S(2)}) collective-permute-start(f32[4,16,512]{2,1,0:T(8,128)S(1)} %get-tuple-element.39), channel_id=1, source_target_pairs={{1,0},{2,1},{3,2},{4,3},{5,4},{6,5},{7,6},{8,7},{9,8},{10,9},{11,1... | collective-permute-start | bytes 393224 | tf_op jit(solution)/shard_map/ppermute | solution.py:708
  8.9 3.6 %inner_advance.1 = (bf16[4,4,96,512]{3,2,1,0:T(8,128)(2,1)S(1)}, f32[96,512]{1,0:T(8,128)S(1)}) custom-call(f32[16,512]{1,0:T(8,128)S(1)} %get-tuple-element.35.table, f32[4,112,256]{2,1,0:T(8,128)S(1)} %get-tuple-element.27.refs_0_, f32[4,112,256]{2,1,0:T(8,128)S(1)} %get-tuple-element.28.refs_1_, f32[4,112,256]{2,1,0:T(8,128)S(1)} %get-tuple-element.29.refs_2_, ...), custom_call_target="tpu_custom_call" | custom-call | flops 10000000000 | bytes 5000000 | tf_op jit(solution)/shard_map/inner_advance/pallas_call | solution.py:290
  12.5 0.0 collective-permute-done.low
  12.6 0.0 collective-permute-done.1.high
  12.6 4.5 %edge_advance.1 = (bf16[4,96,512]{2,1,0:T(8,128)(2,1)}, bf16[4,96,512]{2,1,0:T(8,128)(2,1)}, bf16[4,96,512]{2,1,0:T(8,128)(2,1)}, bf16[4,96,512]{2,1,0:T(8,128)(...) custom-call(bf16[4,4,96,512]{3,2,1,0:T(8,128)(2,1)S(1)} %get-tuple-element.36.staged, ...), custom_call_target="tpu_custom_call" | custom-call | flops 10000000000 | bytes 5000000 | tf_op jit(solution)/shard_map/edge_advance/pallas_call | solution.py:554
  17.1 11.5 %all_to_all.5.sums = f32[16,8,128]{2,1,0:T(8,128)S(1)} all-to-all(f32[16,8,128]{2,1,0:T(8,128)S(1)} %get-tuple-element.44), channel_id=1, replica_groups=mesh['member'=2,'blk'=16] {'blk'}, dimensions={0} | all-to-all | bytes 131072 | tf_op jit(solution)/shard_map/all_to_all | solution.py:713
  28.6 2.7 %combine.1 = (f32[96,512]{1,0:T(8,128)}, f32[96,512]{1,0:T(8,128)}) custom-call(f32[16,8,128]{2,1,0:T(8,128)S(1)} %all_to_all.5.sums, f32[14,144,512]{2,1,0:T(8,128)S(1)} %get-tuple-element.45.fields), custom_call_target="tpu_custom_call" | custom-call | tf_op jit(solution)/shard_map/combine/pallas_call | solution.py:683
Async XLA Ops:
  0.6 2.0 %copy-start = (f32[96,512]{1,0:T(8,128)S(1)}, f32[96,512]{1,0:T(8,128)}, u32[]{:S(2)}) copy-start(f32[96,512]{1,0:T(8,128)} %damp.3) | copy-start | bytes 589828
  0.6 2.0 %copy-start.1 = (s32[1,8]{1,0:T(1,128)S(1)}, s32[1,8]{1,0:T(1,128)}, u32[]{:S(2)}) copy-start(s32[1,8]{1,0:T(1,128)} %flags.1) | copy-start | bytes 100
  0.7 2.0 %copy-start.2 = (f32[4]{0:T(128)S(1)}, f32[4]{0:T(128)}, u32[]{:S(2)}) copy-start(f32[4]{0:T(128)} %param.11) | copy-start | bytes 52
  3.3 9.2 %collective-permute-start = (f32[4,16,512]{2,1,0:T(8,128)S(1)}, f32[4,16,512]{2,1,0:T(8,128)S(1)}, u32[]{:S(2)}, u32[]{:S(2)}) collective-permute-start(f32[4,16,512]{2,1,0:T(8,128)S(1)} %get-tuple-element.38), channel_id=1, source_target_pairs={{0,1},{1,2},{2,3},{3,4},{4,5},{5,6},{6,7},{7,8},{8,9},{9,10},{10,1... | collective-permute-start | bytes 393224 | tf_op jit(solution)/shard_map/ppermute | solution.py:707
  3.9 8.7 %collective-permute-start.1 = (f32[4,16,512]{2,1,0:T(8,128)S(1)}, f32[4,16,512]{2,1,0:T(8,128)S(1)}, u32[]{:S(2)}, u32[]{:S(2)}) collective-permute-start(f32[4,16,512]{2,1,0:T(8,128)S(1)} %get-tuple-element.39), channel_id=1, source_target_pairs={{1,0},{2,1},{3,2},{4,3},{5,4},{6,5},{7,6},{8,7},{9,8},{10,9},{11,1... | collective-permute-start | bytes 393224 | tf_op jit(solution)/shard_map/ppermute | solution.py:708

commit v4 on v3

--- a/solution.py
+++ b/solution.py
@@ -72,8 +72,13 @@
     return east, north
 
 
-def advect(q, east, north, wet):
-    east_flux = upwind(east, q[:-MARGIN], shift(q, -1, 0)[:-MARGIN])
+def east_flow(q, east):
+    return upwind(east, q[:-MARGIN], shift(q, -1, 0)[:-MARGIN])
+
+
+def advect(q, east, north, wet, east_flux=None):
+    if east_flux is None:
+        east_flux = east_flow(q, east)
     centre = q[MARGIN:-MARGIN]
     north_flux = upwind(north, centre, shift(centre, -1, 1))
     spread = (east_flux - shift(east_flux, 1, 0))[MARGIN:] + (
@@ -185,49 +190,52 @@
         message = messages[end]
         rows = slice(0, 2 * PAD) if end == 0 else slice(width - PAD, width + PAD)
 
-        def level_step(k, sums, rows=rows):
+        face = MARGIN - 1 if end == 0 else BASE - 1
+        closed = rows_in((BASE, extent)) == face
+
+        def level_step(k, sums, rows=rows, closed=closed):
             weight = o_table[pl.ds(MARGIN + k, 1)]
             qu = u[k, rows]
             qv = v[k, rows]
             east, north = face_speeds(qu, qv, east_wet, north_wet)
-            au = advect(qu, east, north, wet_row)
-            av = advect(qv, east, north, wet_row)
+            fu = jnp.where(closed, 0.0, east_flow(qu, east))
+            fv = jnp.where(closed, 0.0, east_flow(qv, east))
+            au = advect(qu, east, north, wet_row, fu)
+            av = advect(qv, east, north, wet_row, fv)
             return sums[0] + weight * au, sums[1] + weight * av
 
         zero = jnp.zeros((PAD, extent), jnp.float32)
         flow, cross = lax.fori_loop(0, levels, level_step, (zero, zero), unroll=4)
-        message[0] = divergence(wet_row, flow, cross)
+        start = divergence(wet_row, flow, cross)
         first = 0 if end == 0 else width - PAD
-        message[1] = damp[first : first + PAD]
+        damping = damp[first : first + PAD]
+        near = slice(0, MARGIN) if end == 0 else slice(MARGIN, PAD)
+        far = slice(MARGIN, PAD) if end == 0 else slice(0, MARGIN)
+        message[0] = start[near]
+        message[1] = damping[near]
+        natural = row < 4 if end == 0 else row >= 4
+        message[2] = jnp.where(natural, start[far], shift(damping[far], 4, 0))
         tip = slice(MARGIN, PAD) if end == 0 else slice(width, width + MARGIN)
-        for q in range(2):
+        for slot, pair in ((3, flows), (4, tracers)):
             merged = jnp.zeros((MARGIN, extent), jnp.float32)
-            for k in range(levels):
-                offset = 2 * k if end == 0 else 2 * k + 2 - MARGIN
-                merged = jnp.where(row // 2 == k, shift(flows[q][k, tip], offset, 0), merged)
-            message[2, q * MARGIN : (q + 1) * MARGIN] = merged
-        merged = jnp.zeros((MARGIN, extent), jnp.float32)
-        for q in range(2):
-            for k in range(levels):
-                place = q * levels + k
-                piece = shift(tracers[q][k, tip], place if end == 0 else place + 1, 0)
-                merged = jnp.where(row == place, piece, merged)
-        message[3, 0:MARGIN] = merged
-        if end == 0:
-            flow_piece = shift(flow[:MARGIN], -1, 0)
-            cross_piece = shift(cross[:MARGIN], 1, 0)
-        else:
-            flow_piece = shift(flow[MARGIN:], -5, 0)
-            cross_piece = shift(cross[MARGIN:], -4, 0)
-        message[3, MARGIN:PAD] = jnp.where(
-            row < 2, flow_piece, jnp.where(row == 2, cross_piece, wet)
-        )
+            for q in range(2):
+                for k in range(levels):
+                    place = q * levels + k
+                    piece = shift(pair[q][k, tip], place if end == 0 else place + 1, 0)
+                    merged = jnp.where(row == place, piece, merged)
+            message[slot] = merged
+        flow, cross = flow[near], cross[near]
+        turns = (0, 1, 1, 3) if end == 0 else (1, 2, 5, 6)
+        tail = jnp.where(row == 4, shift(cross, turns[3], 0), wet)
+        tail = jnp.where((row == 2) | (row == 3), shift(flow, turns[2], 0), tail)
+        tail = jnp.where(row == 1, shift(cross, turns[1], 0), tail)
+        message[5] = jnp.where(row == 0, shift(flow, turns[0], 0) if end else flow, tail)
 
 
 def pack(flags, spacing, damp, bands):
     extent = damp.shape[1]
     f32 = jnp.float32
-    message = jax.ShapeDtypeStruct((4, PAD, extent), f32)
+    message = jax.ShapeDtypeStruct((6, MARGIN, extent), f32)
     vmem = pl.BlockSpec(memory_space=pltpu.VMEM)
     return pl.pallas_call(
         pack_kernel,
@@ -336,60 +344,45 @@
     fields[1, BASE : BASE + width] = start_in[...]
 
     for side, message in ((0, low), (1, high)):
-        wet_out = jnp.broadcast_to(message[3, PAD - 1 : PAD], (MARGIN, extent))
+        wet_out = jnp.broadcast_to(message[5, MARGIN - 1 : MARGIN], (MARGIN, extent))
         outer = 0 if side == 0 else BASE + width
         for block in range(BASE // MARGIN):
             ocean[outer + block * MARGIN : outer + (block + 1) * MARGIN] = wet_out
-        halo = MARGIN if side == 0 else BASE + width
         wet_row = wet_out[0:1]
-        diag[halo : halo + PAD] = 0.5 * (
-            wet_row * (6.0 + message[1]) + (1.0 - wet_row)
-        ) - 2.0
+        near = 2 * MARGIN if side == 0 else BASE + width
+        far = MARGIN if side == 0 else BASE + width + MARGIN
+        for at, damping in ((near, message[1]), (far, shift(message[2], 4, 0))):
+            diag[at : at + MARGIN] = 0.5 * (
+                wet_row * (6.0 + damping) + (1.0 - wet_row)
+            ) - 2.0
         if side == 0:
             around = jnp.concatenate([wet_out, wet8, wet8], axis=0)
-            beyond = jnp.concatenate([wet_out, wet_out, wet8], axis=0)
         else:
             around = jnp.concatenate([wet8, wet8, wet_out], axis=0)
-            beyond = jnp.concatenate([wet8, wet_out, wet_out], axis=0)
         east_own = (around * shift(around, -1, 0))[:PAD]
-        east_out = (beyond * shift(beyond, -1, 0))[:PAD]
         north_own = north_wetness(wet8)
-        north_out = north_wetness(wet_out)
 
         mine_at = slice(MARGIN, BASE) if side == 0 else slice(width - MARGIN, width + MARGIN)
         rim_at = slice(0, PAD) if side == 0 else slice(width - PAD, width)
 
         def level_step(k, sums, side=side, message=message, east_own=east_own,
-                       east_out=east_out, north_own=north_own, north_out=north_out,
-                       wet_out=wet_out, mine_at=mine_at, rim_at=rim_at):
+                       north_own=north_own, mine_at=mine_at, rim_at=rim_at):
             weight = table[pl.ds(MARGIN + k, 1)]
-            own, out = [], []
-            for q in (2, 3):
-                place = (q - 2) * MARGIN + 2 * k
-                nearer, farther = message[2, pl.ds(place, 1)], message[2, pl.ds(place + 1, 1)]
-                mine = flows[q - 2][k, mine_at]
-                if side == 0:
-                    piece = jnp.where(row == MARGIN - 1, farther, nearer)
-                    own.append(jnp.concatenate([piece, mine], axis=0))
-                    out.append(jnp.concatenate([piece, piece, mine[:MARGIN]], axis=0))
-                else:
-                    piece = jnp.where(row == 0, nearer, farther)
-                    own.append(jnp.concatenate([mine, piece], axis=0))
-                    out.append(jnp.concatenate([mine[MARGIN:], piece, piece], axis=0))
-            east, north = face_speeds(own[0], own[1], east_own, north_own)
-            au = advect(own[0], east, north, wet8)
-            av = advect(own[1], east, north, wet8)
-            fresh = [None, None, au, av]
-            for q in range(2):
-                mine = tracers[q][k, mine_at]
-                piece = jnp.broadcast_to(
-                    message[3, pl.ds(q * levels + k, 1)], (MARGIN, extent)
-                )
-                if side == 0:
-                    window = jnp.concatenate([piece, mine], axis=0)
-                else:
-                    window = jnp.concatenate([mine, piece], axis=0)
-                fresh[q] = advect(window, east, north, wet8)
+            windows = []
+            for slot, pair in ((4, tracers), (3, flows)):
+                for q in range(2):
+                    mine = pair[q][k, mine_at]
+                    piece = jnp.broadcast_to(
+                        message[slot, pl.ds(q * levels + k, 1)], (MARGIN, extent)
+                    )
+                    pieces = [piece, mine] if side == 0 else [mine, piece]
+                    windows.append(jnp.concatenate(pieces, axis=0))
+            east, north = face_speeds(windows[2], windows[3], east_own, north_own)
+            fluxes = [east_flow(window, east) for window in windows]
+            fresh = [
+                advect(window, east, north, wet8, flux)
+                for window, flux in zip(windows, fluxes)
+            ]
             for q in range(4):
                 old = staged[q, k, rim_at].astype(jnp.float32)
                 if side == 0:
@@ -397,40 +390,43 @@
                 else:
                     value = jnp.concatenate([old[:MARGIN], fresh[q]], axis=0)
                 edge_out[q, side, k] = value.astype(edge_out.dtype)
-            east, north = face_speeds(out[0], out[1], east_out, north_out)
-            bu = advect(out[0], east, north, wet_out)
-            bv = advect(out[1], east, north, wet_out)
+            face_at = slice(0, MARGIN) if side == 0 else slice(MARGIN, PAD)
             return (
-                sums[0] + weight * au,
-                sums[1] + weight * av,
-                sums[2] + weight * bu,
-                sums[3] + weight * bv,
+                sums[0] + weight * fresh[2],
+                sums[1] + weight * fresh[3],
+                sums[2] + weight * fluxes[2][face_at],
+                sums[3] + weight * fluxes[3][face_at],
             )
 
         zero = jnp.zeros((MARGIN, extent), jnp.float32)
-        flow, cross, flow_out, cross_out = lax.fori_loop(
+        flow, cross, flow_face, cross_face = lax.fori_loop(
             0, levels, level_step, (zero, zero, zero, zero), unroll=2
         )
-        known = message[3, MARGIN:PAD]
-        given = message[0]
+        given, farther = message[0], message[2]
+        known = [message[5, i : i + 1] for i in range(5)]
+        change = (-COURANT if side == 0 else COURANT) * wet_out
+        flow_tip = known[0] + change * jnp.broadcast_to(flow_face[MARGIN - 1 :], wet_out.shape)
+        cross_tip = known[1] + change * jnp.broadcast_to(cross_face[MARGIN - 1 :], wet_out.shape)
         if side == 0:
-            flow_out = jnp.where(row == MARGIN - 1, flow_out, shift(known, 5, 0))
-            cross_out = jnp.where(row == MARGIN - 1, cross_out, shift(known, 4, 0))
+            flow_out = jnp.where(row == MARGIN - 2, known[3], known[2])
+            flow_out = jnp.where(row == MARGIN - 1, flow_tip, flow_out)
+            cross_out = jnp.where(row == MARGIN - 1, cross_tip, known[4])
             whole = divergence(
                 jnp.concatenate([wet_out, wet8], axis=0),
                 jnp.concatenate([flow_out, flow], axis=0),
                 jnp.concatenate([cross_out, cross], axis=0),
             )
-            fields[1, MARGIN : 2 * MARGIN] = given[:MARGIN]
+            fields[1, MARGIN : 2 * MARGIN] = farther
             fields[1, 2 * MARGIN : BASE] = jnp.where(
-                row >= MARGIN - 2, whole[:MARGIN], given[MARGIN:]
+                row >= MARGIN - 2, whole[:MARGIN], given
             )
             fields[1, BASE : BASE + MARGIN] = jnp.where(
                 row < 2, whole[MARGIN:], start_in[0:MARGIN]
             )
         else:
-            flow_out = jnp.where(row == 0, flow_out, shift(known, 1, 0))
-            cross_out = jnp.where(row == 0, cross_out, shift(known, -1, 0))
+            flow_out = jnp.where(row == 1, known[2], known[3])
+            flow_out = jnp.where(row == 0, flow_tip, flow_out)
+            cross_out = jnp.where(row == 0, cross_tip, known[4])
             whole = divergence(
                 jnp.concatenate([wet8, wet_out], axis=0),
                 jnp.concatenate([flow, flow_out], axis=0),
@@ -440,8 +436,8 @@
             fields[1, top - MARGIN : top] = jnp.where(
                 row >= MARGIN - 2, whole[:MARGIN], start_in[width - MARGIN : width]
             )
-            fields[1, top : top + MARGIN] = jnp.where(row < 2, whole[MARGIN:], given[:MARGIN])
-            fields[1, top + MARGIN : top + PAD] = given[MARGIN:]
+            fields[1, top : top + MARGIN] = jnp.where(row < 2, whole[MARGIN:], given)
+            fields[1, top + MARGIN : top + PAD] = farther
 
     for q, target in enumerate(targets):
         for side in range(2):
@@ -511,7 +507,7 @@
         basis_step(2 * index + 1, 1, None)
         return carry
 
-    lax.fori_loop(0, STEPS // 2, step_pair, 0)
+    lax.fori_loop(0, STEPS // 2, step_pair, 0, unroll=2)
 
     slots = acc.shape[1] // MARGIN
     pairs = [

time: 31.5 us -> 30.8 us (0.978)
    all_to_all x1, blocking collectives: 11.5 us -> 11.2 us  [on_device(): gathered = lax.all_to_all(sums, 'blk', 0, 0)]
where the time goes in v4:
time: 30.8 us; the launch traced here: 30.6 us
  Pallas kernels  13.2 us (43%)
  blocking collectives  11.2 us (36%)
  starting transfers between devices  5.56 us (18%)
  between operations  0.73 us (2%)
    all_to_all x1, blocking collectives, on_device(): gathered = lax.all_to_all(sums, 'blk', 0, 0)  11.2 us
    ppermute x1, starting transfers between devices, on_device(): high = lax.ppermute(to_last, 'blk', backward)  5.02 us
    pallas_call x1, Pallas kernels, edge_advance(): pl.pallas_call(edge_kernel, out_shape=[tracer] * 4 + [jax.ShapeDtypeStruc...  4.17 us
    pallas_call x1, Pallas kernels, inner_advance(): pl.pallas_call(inner_kernel, out_shape=[jax.ShapeDtypeStruct((4, levels,...  3.62 us
    pallas_call x1, Pallas kernels, combine(): pl.pallas_call(combine_kernel, out_shape=[plane, plane], in_specs=[vmem,...  2.74 us
    pallas_call x1, Pallas kernels, fetch(): pl.pallas_call(fetch_kernel, out_shape=[band] * (4 * PARTS), in_specs=[pl...  1.98 us
    pallas_call x1, Pallas kernels, pack(): pl.pallas_call(pack_kernel, out_shape=[message, message, jax.ShapeDtypeSt...  0.66 us
  transfers between devices with their start and end apart: 2, of which 0 were waited for; matrix products, arithmetic and copies ran while one was open for 0% of the time, Pallas kernels for 12%

profile of v4, /device:TPU:0, one launch (start us, length us, event | category | flops | bytes accessed | tf_op | source)
XLA Modules:
  0.0 30.6 jit_solution(13488793192484243196)
XLA Ops:
  0.6 0.0 copy-start
  0.6 0.0 copy-start.1
  0.7 0.0 copy-start.2
  0.7 2.0 %fetch.1 = (f32[4,112,256]{2,1,0:T(8,128)S(1)}, f32[4,112,256]{2,1,0:T(8,128)S(1)}, f32[4,112,256]{2,1,0:T(8,128)S(1)}, f32[4,112,256]{2,1,0:T(8,128)S(1)}, f32[...) custom-call(f32[4,96,512]{2,1,0:T(8,128)} %heat.1, ...), custom_call_target="tpu_custom_call" | custom-call | flops 10000000000 | bytes 5000000 | tf_op jit(solution)/shard_map/fetch/pallas_call | solution.py:148
  2.6 0.0 copy-done
  2.7 0.0 copy-done.1
  2.7 0.0 copy-done.2
  2.7 0.7 %pack.1 = (f32[6,8,512]{2,1,0:T(8,128)S(1)}, f32[6,8,512]{2,1,0:T(8,128)S(1)}, f32[16,512]{1,0:T(8,128)S(1)}) custom-call(s32[1,8]{1,0:T(1,128)S(1)} %copy-done.1, f32[1,4]{1,0:T(1,128)S(1)} %bitcast.1, f32[96,512]{1,0:T(8,128)S(1)} %copy-done, f32[4,112,256]{2,1,0:T(8,128)S(1)} %get-tuple-element.27.refs_0_, f32[4,112,256]{2,1,0:T(8,128)S(1)} %get-tuple-element.28.refs_1_, ...), custom_call_target="tpu_custom_call" | custom-call | tf_op jit(solution)/shard_map/pack/pallas_call | solution.py:240
  3.3 0.5 %collective-permute-start = (f32[6,8,512]{2,1,0:T(8,128)S(1)}, f32[6,8,512]{2,1,0:T(8,128)S(1)}, u32[]{:S(2)}, u32[]{:S(2)}) collective-permute-start(f32[6,8,512]{2,1,0:T(8,128)S(1)} %get-tuple-element.38), channel_id=1, source_target_pairs={{0,1},{1,2},{2,3},{3,4},{4,5},{5,6},{6,7},{7,8},{8,9},{9,10},{10,1... | collective-permute-start | bytes 294920 | tf_op jit(solution)/shard_map/ppermute | solution.py:703
  3.9 5.0 %collective-permute-start.1 = (f32[6,8,512]{2,1,0:T(8,128)S(1)}, f32[6,8,512]{2,1,0:T(8,128)S(1)}, u32[]{:S(2)}, u32[]{:S(2)}) collective-permute-start(f32[6,8,512]{2,1,0:T(8,128)S(1)} %get-tuple-element.39), channel_id=1, source_target_pairs={{1,0},{2,1},{3,2},{4,3},{5,4},{6,5},{7,6},{8,7},{9,8},{10,9},{11,1... | collective-permute-start | bytes 294920 | tf_op jit(solution)/shard_map/ppermute | solution.py:704
  8.9 3.6 %inner_advance.1 = (bf16[4,4,96,512]{3,2,1,0:T(8,128)(2,1)S(1)}, f32[96,512]{1,0:T(8,128)S(1)}) custom-call(f32[16,512]{1,0:T(8,128)S(1)} %get-tuple-element.35.table, f32[4,112,256]{2,1,0:T(8,128)S(1)} %get-tuple-element.27.refs_0_, f32[4,112,256]{2,1,0:T(8,128)S(1)} %get-tuple-element.28.refs_1_, f32[4,112,256]{2,1,0:T(8,128)S(1)} %get-tuple-element.29.refs_2_, ...), custom_call_target="tpu_custom_call" | custom-call | flops 10000000000 | bytes 5000000 | tf_op jit(solution)/shard_map/inner_advance/pallas_call | solution.py:298
  12.5 0.0 collective-permute-done.low
  12.5 0.0 collective-permute-done.1.high
  12.6 4.2 %edge_advance.1 = (bf16[4,96,512]{2,1,0:T(8,128)(2,1)}, bf16[4,96,512]{2,1,0:T(8,128)(2,1)}, bf16[4,96,512]{2,1,0:T(8,128)(2,1)}, bf16[4,96,512]{2,1,0:T(8,128)(...) custom-call(bf16[4,4,96,512]{3,2,1,0:T(8,128)(2,1)S(1)} %get-tuple-element.36.staged, ...), custom_call_target="tpu_custom_call" | custom-call | flops 10000000000 | bytes 5000000 | tf_op jit(solution)/shard_map/edge_advance/pallas_call | solution.py:550
  16.7 11.2 %all_to_all.5.sums = f32[16,8,128]{2,1,0:T(8,128)S(1)} all-to-all(f32[16,8,128]{2,1,0:T(8,128)S(1)} %get-tuple-element.44), channel_id=1, replica_groups=mesh['member'=2,'blk'=16] {'blk'}, dimensions={0} | all-to-all | bytes 131072 | tf_op jit(solution)/shard_map/all_to_all | solution.py:709
  27.9 2.7 %combine.1 = (f32[96,512]{1,0:T(8,128)}, f32[96,512]{1,0:T(8,128)}) custom-call(f32[16,8,128]{2,1,0:T(8,128)S(1)} %all_to_all.5.sums, f32[14,144,512]{2,1,0:T(8,128)S(1)} %get-tuple-element.45.fields), custom_call_target="tpu_custom_call" | custom-call | tf_op jit(solution)/shard_map/combine/pallas_call | solution.py:679
Async XLA Ops:
  0.6 2.0 %copy-start = (f32[96,512]{1,0:T(8,128)S(1)}, f32[96,512]{1,0:T(8,128)}, u32[]{:S(2)}) copy-start(f32[96,512]{1,0:T(8,128)} %damp.3) | copy-start | bytes 589828
  0.6 2.0 %copy-start.1 = (s32[1,8]{1,0:T(1,128)S(1)}, s32[1,8]{1,0:T(1,128)}, u32[]{:S(2)}) copy-start(s32[1,8]{1,0:T(1,128)} %flags.1) | copy-start | bytes 100
  0.7 2.0 %copy-start.2 = (f32[4]{0:T(128)S(1)}, f32[4]{0:T(128)}, u32[]{:S(2)}) copy-start(f32[4]{0:T(128)} %param.11) | copy-start | bytes 52
  3.3 9.2 %collective-permute-start = (f32[6,8,512]{2,1,0:T(8,128)S(1)}, f32[6,8,512]{2,1,0:T(8,128)S(1)}, u32[]{:S(2)}, u32[]{:S(2)}) collective-permute-start(f32[6,8,512]{2,1,0:T(8,128)S(1)} %get-tuple-element.38), channel_id=1, source_target_pairs={{0,1},{1,2},{2,3},{3,4},{4,5},{5,6},{6,7},{7,8},{8,9},{9,10},{10,1... | collective-permute-start | bytes 294920 | tf_op jit(solution)/shard_map/ppermute | solution.py:703
  3.9 8.7 %collective-permute-start.1 = (f32[6,8,512]{2,1,0:T(8,128)S(1)}, f32[6,8,512]{2,1,0:T(8,128)S(1)}, u32[]{:S(2)}, u32[]{:S(2)}) collective-permute-start(f32[6,8,512]{2,1,0:T(8,128)S(1)} %get-tuple-element.39), channel_id=1, source_target_pairs={{1,0},{2,1},{3,2},{4,3},{5,4},{6,5},{7,6},{8,7},{9,8},{10,9},{11,1... | collective-permute-start | bytes 294920 | tf_op jit(solution)/shard_map/ppermute | solution.py:704

commit v5 on v4

--- a/solution.py
+++ b/solution.py
@@ -16,6 +16,7 @@
 BASE = PAD + MARGIN
 KIB = 1024
 PARTS = 2
+UNROLL = 2
 VMEM_BYTES = 65472 * KIB
 FETCH_ROOM = 14480 * KIB
 PACK_ROOM = 32000 * KIB
@@ -477,15 +478,14 @@
         acc[0, slot * MARGIN : (slot + 1) * MARGIN] = none
         acc[1, slot * MARGIN : (slot + 1) * MARGIN] = none
 
-    def basis_step(j, now, scale):
+    def basis_step(j, now, scale, pieces):
         mixed, square = (none, none), (none, none)
-        for strip in range(strips):
-            start = MARGIN + strip * PAD
-            around = slice(start - MARGIN, start + BASE)
-            keep = slice(start, start + PAD)
+        for start, rows in pieces:
+            around = slice(start - MARGIN, start + rows + MARGIN)
+            keep = slice(start, start + rows)
             wide = masked[now][around]
-            sides = (shift(wide, -1, 0) + shift(wide, 1, 0))[MARGIN:BASE]
-            column = wide[MARGIN:BASE] + 0.5 * sides
+            sides = (shift(wide, -1, 0) + shift(wide, 1, 0))[MARGIN : MARGIN + rows]
+            column = wide[MARGIN : MARGIN + rows] + 0.5 * sides
             near = sides + (north_of(column) + south_of(column))
             centre = fields[j + 1, keep]
             following = diag[keep] * centre - ocean[keep] * near
@@ -494,7 +494,7 @@
             following = following - fields[j, keep]
             fields[j + 2, keep] = following
             masked[1 - now][keep] = half[keep] * following
-            if 0 < strip < strips - 1:
+            if BASE <= start < BASE + width:
                 mixed = inner(centre, following, mixed)
                 square = inner(following, following, square)
         for place, value in ((2 * j + 1, mixed), (2 * j + 2, square)):
@@ -502,12 +502,22 @@
             acc[0, at] = value[0]
             acc[1, at] = value[1]
 
-    def step_pair(index, carry):
-        basis_step(2 * index, 0, jnp.where(index == 0, 0.5, 1.0))
-        basis_step(2 * index + 1, 1, None)
-        return carry
-
-    lax.fori_loop(0, STEPS // 2, step_pair, 0, unroll=2)
+    own = [(BASE + first, PAD) for first in range(0, width, PAD)]
+    whole = [(MARGIN, PAD), *own, (BASE + width, PAD)]
+    short = [(2 * MARGIN, MARGIN), *own, (BASE + width, MARGIN)]
+
+    def step_pair(pieces, first):
+        def run(index, carry):
+            scale = jnp.where(index == 0, 0.5, 1.0) if first else None
+            basis_step(2 * index, 0, scale, pieces)
+            basis_step(2 * index + 1, 1, None, pieces)
+            return carry
+
+        return run
+
+    wide_pairs = -(-(STEPS - MARGIN) // 2)
+    lax.fori_loop(0, wide_pairs, step_pair(whole, True), 0)
+    lax.fori_loop(wide_pairs, STEPS // 2, step_pair(short, False), 0, unroll=UNROLL)
 
     slots = acc.shape[1] // MARGIN
     pairs = [
@@ -534,7 +544,9 @@
         for s in (4, 2, 1):
             merged = merged + shift(merged, s, 0)
         lined.append(merged)
-    o_sums[...] = jnp.broadcast_to(jnp.where(row < 4, lined[0], lined[1])[None], o_sums.shape)
+    packed = jnp.where(place < 64, lined[0], shift(lined[1], 64, 1))
+    for first in range(0, o_sums.shape[0], MARGIN):
+        o_sums[first : first + MARGIN] = packed
     for copy in results:
         copy.wait()
 
@@ -552,7 +564,7 @@
         out_shape=[tracer] * 4
         + [
             jax.ShapeDtypeStruct((STEPS + 2, span, extent), f32),
-            jax.ShapeDtypeStruct((members, MARGIN, 128), f32),
+            jax.ShapeDtypeStruct((members, 128), f32),
         ],
         in_specs=[vmem] * (6 + len(bands)),
         out_specs=[anywhere] * 4 + [vmem] * 2,
@@ -577,8 +589,8 @@
 def combine_kernel(sums, fields, height, resid):
     members = sums.shape[0]
     lane = lax.broadcasted_iota(jnp.int32, (MARGIN, 128), 1)
-    row = lax.broadcasted_iota(jnp.int32, (MARGIN, 128), 0)
-    pieces = [(sums[i], jnp.zeros((MARGIN, 128), jnp.float32)) for i in range(members)]
+    nothing = jnp.zeros((MARGIN, 128), jnp.float32)
+    pieces = [(sums[i : i + MARGIN], nothing) for i in range(0, members, MARGIN)]
     while len(pieces) > 1:
         merged = []
         for x, y in zip(pieces[::2], pieces[1::2]):
@@ -588,13 +600,10 @@
             merged.append(pieces[-1])
         pieces = merged
     total, error = pieces[0]
-    other = shift(total, 4, 0)
-    error_other = shift(error, 4, 0)
-    upper = row < 4
-    dots = fast_two_sum(
-        jnp.where(upper, total, other),
-        jnp.where(upper, other, total) + jnp.where(upper, error, error_other),
-    )
+    for step in (4, 2, 1):
+        total, e = two_sum(total, shift(total, step, 0))
+        error = (error + shift(error, step, 0)) + e
+    dots = fast_two_sum(total, shift(total, 64, 1) + error)
 
     def at(x, k):
         return jnp.broadcast_to(x[:, k : k + 1], x.shape)
@@ -657,8 +666,8 @@
             norm = following
 
     width = height.shape[0]
-    weights_x = [at(c_x, j)[0:1] for j in range(STEPS + 1)]
-    weights_r = [at(c_r[0], j)[0:1] for j in range(STEPS + 1)]
+    weights_x = [at(c_x, j) for j in range(STEPS + 1)]
+    weights_r = [at(c_r[0], j) for j in range(STEPS + 1)]
     for first in range(0, width, MARGIN):
         keep = slice(first, first + MARGIN)
         wide = slice(BASE + first, BASE + first + MARGIN)
@@ -706,7 +715,7 @@
     *tracers, basis, sums = edge_advance(
         staged, start, diagonal_shift, table, low, high, bands, members
     )
-    gathered = lax.all_to_all(sums, "blk", 0, 0)
+    gathered = lax.all_to_all(sums, "blk", 0, 0, tiled=True)
     height, resid = combine(gathered, basis, diagonal_shift.shape[0])
     return (*tracers, height, resid)
 

time: 30.8 us -> 30.3 us (0.984)
  blocking collectives: 11.2 us -> 10.7 us
    all_to_all x1, blocking collectives: 11.2 us -> 10.7 us  [on_device(): gathered = lax.all_to_all(sums, 'blk', 0, 0, tiled=True)]
where the time goes in v5:
time: 30.3 us; the launch traced here: 30.1 us
  Pallas kernels  13.1 us (43%)
  blocking collectives  10.7 us (35%)
  starting transfers between devices  5.56 us (18%)
  between operations  0.73 us (2%)
    all_to_all x1, blocking collectives, on_device(): gathered = lax.all_to_all(sums, 'blk', 0, 0, tiled=True)  10.7 us
    ppermute x1, starting transfers between devices, on_device(): high = lax.ppermute(to_last, 'blk', backward)  5.02 us
    pallas_call x1, Pallas kernels, edge_advance(): pl.pallas_call(edge_kernel, out_shape=[tracer] * 4 + [jax.ShapeDtypeStruc...  4.1 us
    pallas_call x1, Pallas kernels, inner_advance(): pl.pallas_call(inner_kernel, out_shape=[jax.ShapeDtypeStruct((4, levels,...  3.62 us
    pallas_call x1, Pallas kernels, combine(): pl.pallas_call(combine_kernel, out_shape=[plane, plane], in_specs=[vmem,...  2.76 us
    pallas_call x1, Pallas kernels, fetch(): pl.pallas_call(fetch_kernel, out_shape=[band] * (4 * PARTS), in_specs=[pl...  1.98 us
    pallas_call x1, Pallas kernels, pack(): pl.pallas_call(pack_kernel, out_shape=[message, message, jax.ShapeDtypeSt...  0.66 us
  transfers between devices with their start and end apart: 2, of which 0 were waited for; matrix products, arithmetic and copies ran while one was open for 0% of the time, Pallas kernels for 12%

profile of v5, /device:TPU:0, one launch (start us, length us, event | category | flops | bytes accessed | tf_op | source)
XLA Modules:
  0.0 30.1 jit_solution(15478418031088739868)
XLA Ops:
  0.6 0.0 copy-start
  0.6 0.0 copy-start.1
  0.7 0.0 copy-start.2
  0.7 2.0 %fetch.1 = (f32[4,112,256]{2,1,0:T(8,128)S(1)}, f32[4,112,256]{2,1,0:T(8,128)S(1)}, f32[4,112,256]{2,1,0:T(8,128)S(1)}, f32[4,112,256]{2,1,0:T(8,128)S(1)}, f32[...) custom-call(f32[4,96,512]{2,1,0:T(8,128)} %heat.1, ...), custom_call_target="tpu_custom_call" | custom-call | flops 10000000000 | bytes 5000000 | tf_op jit(solution)/shard_map/fetch/pallas_call | solution.py:149
  2.6 0.0 copy-done
  2.7 0.0 copy-done.1
  2.7 0.0 copy-done.2
  2.7 0.7 %pack.1 = (f32[6,8,512]{2,1,0:T(8,128)S(1)}, f32[6,8,512]{2,1,0:T(8,128)S(1)}, f32[16,512]{1,0:T(8,128)S(1)}) custom-call(s32[1,8]{1,0:T(1,128)S(1)} %copy-done.1, f32[1,4]{1,0:T(1,128)S(1)} %bitcast.7, f32[96,512]{1,0:T(8,128)S(1)} %copy-done, f32[4,112,256]{2,1,0:T(8,128)S(1)} %get-tuple-element.27.refs_0_, f32[4,112,256]{2,1,0:T(8,128)S(1)} %get-tuple-element.28.refs_1_, ...), custom_call_target="tpu_custom_call" | custom-call | tf_op jit(solution)/shard_map/pack/pallas_call | solution.py:241
  3.3 0.5 %collective-permute-start = (f32[6,8,512]{2,1,0:T(8,128)S(1)}, f32[6,8,512]{2,1,0:T(8,128)S(1)}, u32[]{:S(2)}, u32[]{:S(2)}) collective-permute-start(f32[6,8,512]{2,1,0:T(8,128)S(1)} %get-tuple-element.38), channel_id=1, source_target_pairs={{0,1},{1,2},{2,3},{3,4},{4,5},{5,6},{6,7},{7,8},{8,9},{9,10},{10,1... | collective-permute-start | bytes 294920 | tf_op jit(solution)/shard_map/ppermute | solution.py:712
  3.9 5.0 %collective-permute-start.1 = (f32[6,8,512]{2,1,0:T(8,128)S(1)}, f32[6,8,512]{2,1,0:T(8,128)S(1)}, u32[]{:S(2)}, u32[]{:S(2)}) collective-permute-start(f32[6,8,512]{2,1,0:T(8,128)S(1)} %get-tuple-element.39), channel_id=1, source_target_pairs={{1,0},{2,1},{3,2},{4,3},{5,4},{6,5},{7,6},{8,7},{9,8},{10,9},{11,1... | collective-permute-start | bytes 294920 | tf_op jit(solution)/shard_map/ppermute | solution.py:713
  8.9 3.6 %inner_advance.1 = (bf16[4,4,96,512]{3,2,1,0:T(8,128)(2,1)S(1)}, f32[96,512]{1,0:T(8,128)S(1)}) custom-call(f32[16,512]{1,0:T(8,128)S(1)} %get-tuple-element.35.table, f32[4,112,256]{2,1,0:T(8,128)S(1)} %get-tuple-element.27.refs_0_, f32[4,112,256]{2,1,0:T(8,128)S(1)} %get-tuple-element.28.refs_1_, f32[4,112,256]{2,1,0:T(8,128)S(1)} %get-tuple-element.29.refs_2_, ...), custom_call_target="tpu_custom_call" | custom-call | flops 10000000000 | bytes 5000000 | tf_op jit(solution)/shard_map/inner_advance/pallas_call | solution.py:299
  12.5 0.0 collective-permute-done.low
  12.5 0.0 collective-permute-done.1.high
  12.6 4.1 %edge_advance.1 = (bf16[4,96,512]{2,1,0:T(8,128)(2,1)}, bf16[4,96,512]{2,1,0:T(8,128)(2,1)}, bf16[4,96,512]{2,1,0:T(8,128)(2,1)}, bf16[4,96,512]{2,1,0:T(8,128)(...) custom-call(bf16[4,4,96,512]{3,2,1,0:T(8,128)(2,1)S(1)} %get-tuple-element.36.staged, ...), custom_call_target="tpu_custom_call" | custom-call | flops 10000000000 | bytes 5000000 | tf_op jit(solution)/shard_map/edge_advance/pallas_call | solution.py:562
  16.7 10.7 %all_to_all.11 = f32[16,1,128]{2,1,0:T(1,128)S(1)} all-to-all(f32[16,1,128]{2,1,0:T(1,128)S(1)} %bitcast.6), channel_id=1, replica_groups=mesh['member'=2,'blk'=16] {'blk'}, dimensions={0} | all-to-all | bytes 16384 | tf_op jit(solution)/shard_map/all_to_all | solution.py:718
  27.4 2.8 %combine.1 = (f32[96,512]{1,0:T(8,128)}, f32[96,512]{1,0:T(8,128)}) custom-call(f32[16,128]{1,0:T(8,128)S(1)} %bitcast.5, f32[14,144,512]{2,1,0:T(8,128)S(1)} %get-tuple-element.45.fields), custom_call_target="tpu_custom_call" | custom-call | tf_op jit(solution)/shard_map/combine/pallas_call | solution.py:688
Async XLA Ops:
  0.6 2.0 %copy-start = (f32[96,512]{1,0:T(8,128)S(1)}, f32[96,512]{1,0:T(8,128)}, u32[]{:S(2)}) copy-start(f32[96,512]{1,0:T(8,128)} %damp.3) | copy-start | bytes 589828
  0.6 2.0 %copy-start.1 = (s32[1,8]{1,0:T(1,128)S(1)}, s32[1,8]{1,0:T(1,128)}, u32[]{:S(2)}) copy-start(s32[1,8]{1,0:T(1,128)} %flags.1) | copy-start | bytes 100
  0.7 2.0 %copy-start.2 = (f32[4]{0:T(128)S(1)}, f32[4]{0:T(128)}, u32[]{:S(2)}) copy-start(f32[4]{0:T(128)} %param.11) | copy-start | bytes 52
  3.3 9.2 %collective-permute-start = (f32[6,8,512]{2,1,0:T(8,128)S(1)}, f32[6,8,512]{2,1,0:T(8,128)S(1)}, u32[]{:S(2)}, u32[]{:S(2)}) collective-permute-start(f32[6,8,512]{2,1,0:T(8,128)S(1)} %get-tuple-element.38), channel_id=1, source_target_pairs={{0,1},{1,2},{2,3},{3,4},{4,5},{5,6},{6,7},{7,8},{8,9},{9,10},{10,1... | collective-permute-start | bytes 294920 | tf_op jit(solution)/shard_map/ppermute | solution.py:712
  3.9 8.7 %collective-permute-start.1 = (f32[6,8,512]{2,1,0:T(8,128)S(1)}, f32[6,8,512]{2,1,0:T(8,128)S(1)}, u32[]{:S(2)}, u32[]{:S(2)}) collective-permute-start(f32[6,8,512]{2,1,0:T(8,128)S(1)} %get-tuple-element.39), channel_id=1, source_target_pairs={{1,0},{2,1},{3,2},{4,3},{5,4},{6,5},{7,6},{8,7},{9,8},{10,9},{11,1... | collective-permute-start | bytes 294920 | tf_op jit(solution)/shard_map/ppermute | solution.py:713

commit v6 on v5

--- a/solution.py
+++ b/solution.py
@@ -516,7 +516,7 @@
         return run
 
     wide_pairs = -(-(STEPS - MARGIN) // 2)
-    lax.fori_loop(0, wide_pairs, step_pair(whole, True), 0)
+    lax.fori_loop(0, wide_pairs, step_pair(whole, True), 0, unroll=UNROLL)
     lax.fori_loop(wide_pairs, STEPS // 2, step_pair(short, False), 0, unroll=UNROLL)
 
     slots = acc.shape[1] // MARGIN

time: 30.3 us -> 30.2 us (level)
  no operation moved by 1% of the time
where the time goes in v6:
time: 30.2 us; the launch traced here: 30 us
  Pallas kernels  13 us (43%)
  blocking collectives  10.7 us (35%)
  starting transfers between devices  5.56 us (18%)
  between operations  0.73 us (2%)
    all_to_all x1, blocking collectives, on_device(): gathered = lax.all_to_all(sums, 'blk', 0, 0, tiled=True)  10.7 us
    ppermute x1, starting transfers between devices, on_device(): high = lax.ppermute(to_last, 'blk', backward)  5.02 us
    pallas_call x1, Pallas kernels, edge_advance(): pl.pallas_call(edge_kernel, out_shape=[tracer] * 4 + [jax.ShapeDtypeStruc...  4.01 us
    pallas_call x1, Pallas kernels, inner_advance(): pl.pallas_call(inner_kernel, out_shape=[jax.ShapeDtypeStruct((4, levels,...  3.62 us
    pallas_call x1, Pallas kernels, combine(): pl.pallas_call(combine_kernel, out_shape=[plane, plane], in_specs=[vmem,...  2.76 us
    pallas_call x1, Pallas kernels, fetch(): pl.pallas_call(fetch_kernel, out_shape=[band] * (4 * PARTS), in_specs=[pl...  1.98 us
    pallas_call x1, Pallas kernels, pack(): pl.pallas_call(pack_kernel, out_shape=[message, message, jax.ShapeDtypeSt...  0.66 us
  transfers between devices with their start and end apart: 2, of which 0 were waited for; matrix products, arithmetic and copies ran while one was open for 0% of the time, Pallas kernels for 12%

profile of v6, /device:TPU:0, one launch (start us, length us, event | category | flops | bytes accessed | tf_op | source)
XLA Modules:
  0.0 30.0 jit_solution(886119130448285271)
XLA Ops:
  0.6 0.0 copy-start
  0.6 0.0 copy-start.1
  0.7 0.0 copy-start.2
  0.7 2.0 %fetch.1 = (f32[4,112,256]{2,1,0:T(8,128)S(1)}, f32[4,112,256]{2,1,0:T(8,128)S(1)}, f32[4,112,256]{2,1,0:T(8,128)S(1)}, f32[4,112,256]{2,1,0:T(8,128)S(1)}, f32[...) custom-call(f32[4,96,512]{2,1,0:T(8,128)} %heat.1, ...), custom_call_target="tpu_custom_call" | custom-call | flops 10000000000 | bytes 5000000 | tf_op jit(solution)/shard_map/fetch/pallas_call | solution.py:149
  2.6 0.0 copy-done
  2.7 0.0 copy-done.1
  2.7 0.0 copy-done.2
  2.7 0.7 %pack.1 = (f32[6,8,512]{2,1,0:T(8,128)S(1)}, f32[6,8,512]{2,1,0:T(8,128)S(1)}, f32[16,512]{1,0:T(8,128)S(1)}) custom-call(s32[1,8]{1,0:T(1,128)S(1)} %copy-done.1, f32[1,4]{1,0:T(1,128)S(1)} %bitcast.7, f32[96,512]{1,0:T(8,128)S(1)} %copy-done, f32[4,112,256]{2,1,0:T(8,128)S(1)} %get-tuple-element.27.refs_0_, f32[4,112,256]{2,1,0:T(8,128)S(1)} %get-tuple-element.28.refs_1_, ...), custom_call_target="tpu_custom_call" | custom-call | tf_op jit(solution)/shard_map/pack/pallas_call | solution.py:241
  3.3 0.5 %collective-permute-start = (f32[6,8,512]{2,1,0:T(8,128)S(1)}, f32[6,8,512]{2,1,0:T(8,128)S(1)}, u32[]{:S(2)}, u32[]{:S(2)}) collective-permute-start(f32[6,8,512]{2,1,0:T(8,128)S(1)} %get-tuple-element.38), channel_id=1, source_target_pairs={{0,1},{1,2},{2,3},{3,4},{4,5},{5,6},{6,7},{7,8},{8,9},{9,10},{10,1... | collective-permute-start | bytes 294920 | tf_op jit(solution)/shard_map/ppermute | solution.py:712
  3.9 5.0 %collective-permute-start.1 = (f32[6,8,512]{2,1,0:T(8,128)S(1)}, f32[6,8,512]{2,1,0:T(8,128)S(1)}, u32[]{:S(2)}, u32[]{:S(2)}) collective-permute-start(f32[6,8,512]{2,1,0:T(8,128)S(1)} %get-tuple-element.39), channel_id=1, source_target_pairs={{1,0},{2,1},{3,2},{4,3},{5,4},{6,5},{7,6},{8,7},{9,8},{10,9},{11,1... | collective-permute-start | bytes 294920 | tf_op jit(solution)/shard_map/ppermute | solution.py:713
  8.9 3.6 %inner_advance.1 = (bf16[4,4,96,512]{3,2,1,0:T(8,128)(2,1)S(1)}, f32[96,512]{1,0:T(8,128)S(1)}) custom-call(f32[16,512]{1,0:T(8,128)S(1)} %get-tuple-element.35.table, f32[4,112,256]{2,1,0:T(8,128)S(1)} %get-tuple-element.27.refs_0_, f32[4,112,256]{2,1,0:T(8,128)S(1)} %get-tuple-element.28.refs_1_, f32[4,112,256]{2,1,0:T(8,128)S(1)} %get-tuple-element.29.refs_2_, ...), custom_call_target="tpu_custom_call" | custom-call | flops 10000000000 | bytes 5000000 | tf_op jit(solution)/shard_map/inner_advance/pallas_call | solution.py:299
  12.5 0.0 collective-permute-done.low
  12.5 0.0 collective-permute-done.1.high
  12.6 4.0 %edge_advance.1 = (bf16[4,96,512]{2,1,0:T(8,128)(2,1)}, bf16[4,96,512]{2,1,0:T(8,128)(2,1)}, bf16[4,96,512]{2,1,0:T(8,128)(2,1)}, bf16[4,96,512]{2,1,0:T(8,128)(...) custom-call(bf16[4,4,96,512]{3,2,1,0:T(8,128)(2,1)S(1)} %get-tuple-element.36.staged, ...), custom_call_target="tpu_custom_call" | custom-call | flops 10000000000 | bytes 5000000 | tf_op jit(solution)/shard_map/edge_advance/pallas_call | solution.py:562
  16.6 10.7 %all_to_all.11 = f32[16,1,128]{2,1,0:T(1,128)S(1)} all-to-all(f32[16,1,128]{2,1,0:T(1,128)S(1)} %bitcast.6), channel_id=1, replica_groups=mesh['member'=2,'blk'=16] {'blk'}, dimensions={0} | all-to-all | bytes 16384 | tf_op jit(solution)/shard_map/all_to_all | solution.py:718
  27.3 2.8 %combine.1 = (f32[96,512]{1,0:T(8,128)}, f32[96,512]{1,0:T(8,128)}) custom-call(f32[16,128]{1,0:T(8,128)S(1)} %bitcast.5, f32[14,144,512]{2,1,0:T(8,128)S(1)} %get-tuple-element.45.fields), custom_call_target="tpu_custom_call" | custom-call | tf_op jit(solution)/shard_map/combine/pallas_call | solution.py:688
Async XLA Ops:
  0.6 2.0 %copy-start = (f32[96,512]{1,0:T(8,128)S(1)}, f32[96,512]{1,0:T(8,128)}, u32[]{:S(2)}) copy-start(f32[96,512]{1,0:T(8,128)} %damp.3) | copy-start | bytes 589828
  0.6 2.0 %copy-start.1 = (s32[1,8]{1,0:T(1,128)S(1)}, s32[1,8]{1,0:T(1,128)}, u32[]{:S(2)}) copy-start(s32[1,8]{1,0:T(1,128)} %flags.1) | copy-start | bytes 100
  0.7 2.0 %copy-start.2 = (f32[4]{0:T(128)S(1)}, f32[4]{0:T(128)}, u32[]{:S(2)}) copy-start(f32[4]{0:T(128)} %param.11) | copy-start | bytes 52
  3.3 9.2 %collective-permute-start = (f32[6,8,512]{2,1,0:T(8,128)S(1)}, f32[6,8,512]{2,1,0:T(8,128)S(1)}, u32[]{:S(2)}, u32[]{:S(2)}) collective-permute-start(f32[6,8,512]{2,1,0:T(8,128)S(1)} %get-tuple-element.38), channel_id=1, source_target_pairs={{0,1},{1,2},{2,3},{3,4},{4,5},{5,6},{6,7},{7,8},{8,9},{9,10},{10,1... | collective-permute-start | bytes 294920 | tf_op jit(solution)/shard_map/ppermute | solution.py:712
  3.9 8.7 %collective-permute-start.1 = (f32[6,8,512]{2,1,0:T(8,128)S(1)}, f32[6,8,512]{2,1,0:T(8,128)S(1)}, u32[]{:S(2)}, u32[]{:S(2)}) collective-permute-start(f32[6,8,512]{2,1,0:T(8,128)S(1)} %get-tuple-element.39), channel_id=1, source_target_pairs={{1,0},{2,1},{3,2},{4,3},{5,4},{6,5},{7,6},{8,7},{9,8},{10,9},{11,1... | collective-permute-start | bytes 294920 | tf_op jit(solution)/shard_map/ppermute | solution.py:713
